TPU v7x, 32 devices: a 4x4x1 block of a 4x4x8 slice. The times are simulated.
32 devices in a mesh: rep: 1 (over z), r: 4 (over y), s: 8 (over x, core).
Axes of the slice: x: 4, y: 4, z: 1, core: 2. Of those that a mesh axis runs over, the one named last changes fastest.
The devices are a block of a 4x4x8 slice.
Arguments:
- x: bfloat16 [32, 2048, 896], P(('rep', 'r', 's'))
- dy: bfloat16 [32, 2048, 896], P(('rep', 'r', 's'))
- w_gate: bfloat16 [2, 896, 3584], P(None, 's')
- w_up: bfloat16 [2, 896, 3584], P(None, 's')
- w_down: bfloat16 [2, 3584, 896], P(None, 's')
Outputs:
- output 1: bfloat16 [32, 2048, 896], P(('rep', 'r', 's'))
- output 2: bfloat16 [2, 896, 3584], P('rep', 's')
- output 3: bfloat16 [2, 896, 3584], P('rep', 's')
- output 4: bfloat16 [2, 3584, 896], P('rep', 's')
All inputs are finite; a program needn't handle non-finite values.
Results may differ from a plain program's by a relative error of at most 0.018.
Values are sent between devices in bfloat16 or wider.
A program may use at most 768 MiB of HBM per device.

v0:
```python
import jax
import jax.numpy as jnp
from jax import lax
from jax.sharding import PartitionSpec as P

NAMES = ("w_gate", "w_up", "w_down")


def matmul(a, w):
    return jnp.dot(a, w, preferred_element_type=jnp.float32).astype(jnp.bfloat16)


def normed(h):
    wide = h.astype(jnp.float32)
    scale = lax.rsqrt(jnp.mean(wide**2, -1, keepdims=True) + 1e-6)
    return (wide * scale).astype(jnp.bfloat16)


def layer(h, w):
    a = normed(h)
    gate = jnp.dot(a, w["w_gate"], preferred_element_type=jnp.float32)
    up = jnp.dot(a, w["w_up"], preferred_element_type=jnp.float32)
    return h + matmul((jax.nn.silu(gate) * up).astype(jnp.bfloat16), w["w_down"])


def solution(mesh):
    def fetched(weights, number):
        return {name: lax.all_gather(w[number], "s", axis=0, tiled=True) for name, w in zip(NAMES, weights, strict=True)}

    def summed(term):
        return lax.psum(lax.psum_scatter(term, "s", scatter_dimension=0, tiled=True), "r")

    def step(x, dy, *weights):
        layers = weights[0].shape[0]
        h, inputs = x[0], []
        for number in range(layers):
            inputs.append(h)
            h = layer(h, fetched(weights, number))
        by_h, mine = dy[0], [None] * layers
        for number in reversed(range(layers)):
            _, back = jax.vjp(lambda w, h: layer(h, w), fetched(weights, number), inputs[number])
            by_w, by_h = back(by_h)
            mine[number] = [summed(by_w[name]) for name in NAMES]
        return (by_h[None], *(jnp.stack([mine[number][i] for number in range(layers)]) for i in range(3)))

    states, cut = P(("rep", "r", "s"), None, None), P(None, "s", None)
    return jax.shard_map(
        step,
        mesh=mesh,
        in_specs=(states, states) + (cut,) * 3,
        out_specs=(states,) + (P("rep", "s", None),) * 3,
        check_vma=False,
    )
```

profile of v0, /device:TPU:97, one launch (start us, length us, event | category | flops | bytes accessed | tf_op | source)
XLA Modules:
  0.0 740.3 jit_solution(16232103975222493623)
XLA Ops:
  31.9 21.2 %all-gather.13.cloned.1.call-done = bf16[1,896,3584]{2,1,0:T(8,128)(2,1)} async-done(((bf16[1,112,3584]{2,1,0:T(8,128)(2,1)}), bf16[1,896,3584]{2,1,0:T(8,128)(2,1)}) %all-gather.13.cloned.1.call-update) | async-done | bytes 6422544 | tf_op jit(solution)/shard_map/all_gather | solution.py:28
  53.1 24.1 %fusion.40 = f32[2048,3584]{1,0:T(8,128)} fusion(bf16[1,896,3584]{2,1,0:T(8,128)(2,1)} %all-gather.13.cloned.1.call-done, bf16[1,2048,896]{1,2,0:T(8,128)(2,1)} %copy.10, f32[2048]{0:T(1024)S(1)} %fusion.61), kind=kOutput, calls=%fused_computation.65 | convolution fusion | flops 13158842368 | bytes 39460864 | tf_op jit(solution)/shard_map/dot_general | solution.py:21
  93.5 34.1 %multiply_convert_fusion.1 = (bf16[2048,3584]{1,0:T(8,128)(2,1)}, f32[2048,3584]{1,0:T(8,128)}) fusion(f32[2048,3584]{1,0:T(8,128)} %fusion.40, bf16[1,896,3584]{2,1,0:T(8,128)(2,1)} %all-gather.15.cloned.1.call-done, bf16[1,2048,896]{1,2,0:T(8,128)(2,1)} %copy.10, f32[2048]{0:T(1024)S(1)} %fusion.61), kind=kOutput, calls=%fused_computation.13 | convolution fusion | flops 13202882560 | bytes 83501056 | tf_op jit(solution)/shard_map/dot_general | solution.py:22
  133.9 21.1 %fusion.18 = (f32[2048]{0:T(1024)S(1)}, bf16[2048,896]{0,1:T(8,128)(2,1)}) fusion(bf16[2048,3584]{1,0:T(8,128)(2,1)} %get-tuple-element.20, bf16[1,3584,896]{2,1,0:T(8,128)(2,1)} %all-gather.17.cloned.1.call-done, bf16[1,2048,896]{1,2,0:T(8,128)(2,1)} %copy.10), kind=kOutput, calls=%fused_computation.40 | convolution fusion | flops 13162510336 | bytes 28450816 | tf_op jit(solution)/shard_map/dot_general | solution.py:10
  155.0 19.1 %all-gather.21.cloned.1.call-done = bf16[1,3584,896]{2,1,0:T(8,128)(2,1)} async-done(((bf16[1,448,896]{2,1,0:T(8,128)(2,1)}), bf16[1,3584,896]{2,1,0:T(8,128)(2,1)}) %all-gather.21.cloned.1.call-update) | async-done | bytes 6422544 | tf_op jit(solution)/shard_map/all_gather | solution.py:28
  174.1 22.1 %convolution_convert_fusion.1 = bf16[2048,3584]{1,0:T(8,128)(2,1)} fusion(bf16[1,3584,896]{2,1,0:T(8,128)(2,1)} %all-gather.21.cloned.1.call-done, bf16[1,2048,896]{2,1,0:T(8,128)(2,1)} %param.6), kind=kOutput, calls=%fused_computation.21 | convolution fusion | flops 13160677376 | bytes 24772608 | tf_op jit(solution)/shard_map/transpose(jvp())/dot_general | solution.py:10
  196.2 18.7 %all-gather.23.cloned.1.call-done = bf16[1,896,3584]{2,1,0:T(8,128)(2,1)} async-done(((bf16[1,112,3584]{2,1,0:T(8,128)(2,1)}), bf16[1,896,3584]{2,1,0:T(8,128)(2,1)}) %all-gather.23.cloned.1.call-update) | async-done | bytes 6422544 | tf_op jit(solution)/shard_map/all_gather | solution.py:28
  214.9 24.0 %fusion.24 = f32[2048,3584]{1,0:T(8,128)} fusion(bf16[1,896,3584]{2,1,0:T(8,128)(2,1)} %all-gather.23.cloned.1.call-done, bf16[2048,896]{0,1:T(8,128)(2,1)} %get-tuple-element.23, f32[2048]{0:T(1024)S(1)} %fusion.62), kind=kOutput, calls=%fused_computation.49 | convolution fusion | flops 13158842368 | bytes 39460864 | tf_op jit(solution)/shard_map/jvp()/dot_general | solution.py:22
  255.7 43.1 %fusion.1 = (bf16[2048,3584]{1,0:T(8,128)(2,1)}, f32[2048,3584]{1,0:T(8,128)}) fusion(f32[2048,3584]{1,0:T(8,128)} %fusion.24, bf16[2048,3584]{1,0:T(8,128)(2,1)} %convolution_convert_fusion.1, bf16[1,896,3584]{2,1,0:T(8,128)(2,1)} %all-gather.19.cloned.1.call-done, bf16[2048,896]{0,1:T(8,128)(2,1)} %get-tuple-element.23, f32[2048]{0:T(1024)S(1)} %fusion.62), kind=kOutput, calls=%fused_computation.7 | convolution fusion | flops 13246922752 | bytes 98181120 | tf_op jit(solution)/shard_map/jvp()/dot_general | solution.py:21
  298.8 22.7 %fusion.7 = bf16[2048,896]{0,1:T(8,128)(2,1)} fusion(bf16[2048,3584]{1,0:T(8,128)(2,1)} %convolution_convert_fusion.1, bf16[1,896,3584]{2,1,0:T(8,128)(2,1)} %all-gather.23.cloned.1.call-done, f32[2048,3584]{1,0:T(8,128)} %get-tuple-element.25), kind=kOutput, calls=%fused_computation.17 | convolution fusion | flops 13197377536 | bytes 54132736 | tf_op jit(solution)/shard_map/transpose(jvp())/dot_general | solution.py:22
  321.5 19.9 %fusion.20 = (f32[2048]{0:T(1024)S(1)}, bf16[2048,896]{0,1:T(8,128)(2,1)S(1)}) fusion(bf16[2048,896]{0,1:T(8,128)(2,1)S(1)} %copy-done.4, bf16[2048,896]{0,1:T(8,128)(2,1)} %fusion.7, bf16[2048,3584]{1,0:T(8,128)(2,1)} %get-tuple-element.24, bf16[1,896,3584]{2,1,0:T(8,128)(2,1)} %all-gather.19.cloned.1.call-done), kind=kOutput, calls=%fused_computation.42 | convolution fusion | flops 13162510336 | bytes 32120832 | tf_op jit(solution)/shard_map/transpose(jvp())/dot_general | solution.py:21
  346.3 19.4 %convolution_convert_fusion.2 = bf16[3584,896]{1,0:T(8,128)(2,1)} fusion(bf16[2048,3584]{1,0:T(8,128)(2,1)} %get-tuple-element.20, bf16[2048,896]{0,1:T(8,128)(2,1)S(1)} %fusion.44), kind=kOutput, calls=%fused_computation.46 | convolution fusion | flops 13156548608 | bytes 24772608 | tf_op jit(solution)/shard_map/transpose(jvp())/dot_general | solution.py:10
  365.8 26.7 %fusion.21 = bf16[3584,896]{1,0:T(8,128)(2,1)} fusion(f32[2048,3584]{1,0:T(8,128)} %fusion.24, bf16[1,2048,896]{2,1,0:T(8,128)(2,1)} %param.6, f32[2048,3584]{1,0:T(8,128)} %get-tuple-element.25), kind=kOutput, calls=%fused_computation.43 | convolution fusion | flops 13200588800 | bytes 68812800 | tf_op jit(solution)/shard_map/transpose(jvp())/dot_general | solution.py:10
  392.6 42.1 %fusion.3 = (bf16[2048,3584]{1,0:T(8,128)(2,1)}, bf16[2048,3584]{1,0:T(8,128)(2,1)}) fusion(f32[2048,3584]{1,0:T(8,128)} %fusion.40, f32[2048,3584]{1,0:T(8,128)} %get-tuple-element.21, bf16[2048,896]{0,1:T(8,128)(2,1)} %copy-done.2, bf16[1,3584,896]{2,1,0:T(8,128)(2,1)} %all-gather.17.cloned.1.call-done), kind=kOutput, calls=%fused_computation.9 | convolution fusion | flops 13248757760 | bytes 98172928 | tf_op jit(solution)/shard_map/transpose(jvp())/dot_general | solution.py:10
  434.8 24.0 %fusion.22 = bf16[896,3584]{1,0:T(8,128)(2,1)} fusion(bf16[2048,3584]{1,0:T(8,128)(2,1)} %get-tuple-element.29, bf16[1,2048,896]{1,2,0:T(8,128)(2,1)} %copy.10, f32[2048]{0:T(1024)S(1)} %copy-done.9, f32[2048,3584]{1,0:T(8,128)} %fusion.40), kind=kOutput, calls=%fused_computation.44 | convolution fusion | flops 13206093824 | bytes 54140928 | tf_op jit(solution)/shard_map/transpose(jvp())/dot_general | solution.py:22
  458.9 24.1 %fusion.23 = bf16[896,3584]{1,0:T(8,128)(2,1)} fusion(bf16[2048,3584]{1,0:T(8,128)(2,1)} %convolution_convert_fusion.1, bf16[2048,896]{0,1:T(8,128)(2,1)} %get-tuple-element.23, f32[2048]{0:T(1024)S(1)} %copy-done.11, f32[2048,3584]{1,0:T(8,128)} %get-tuple-element.25), kind=kOutput, calls=%fused_computation.45 | convolution fusion | flops 13206093824 | bytes 54140928 | tf_op jit(solution)/shard_map/transpose(jvp())/dot_general | solution.py:22
  483.1 19.4 %convolution_convert_fusion.3 = bf16[896,3584]{1,0:T(8,128)(2,1)} fusion(bf16[2048,3584]{1,0:T(8,128)(2,1)} %get-tuple-element.24, bf16[2048,896]{0,1:T(8,128)(2,1)} %get-tuple-element.23, f32[2048]{0:T(1024)S(1)} %copy-done.11), kind=kOutput, calls=%fused_computation.47 | convolution fusion | flops 13158842368 | bytes 24780800 | tf_op jit(solution)/shard_map/transpose(jvp())/dot_general | solution.py:21
  502.7 19.4 %convolution_convert_fusion.4 = bf16[896,3584]{1,0:T(8,128)(2,1)} fusion(bf16[2048,3584]{1,0:T(8,128)(2,1)} %get-tuple-element.28, bf16[1,2048,896]{1,2,0:T(8,128)(2,1)} %copy.10, f32[2048]{0:T(1024)S(1)} %copy-done.9), kind=kOutput, calls=%fused_computation.48 | convolution fusion | flops 13158842368 | bytes 24780800 | tf_op jit(solution)/shard_map/transpose(jvp())/dot_general | solution.py:21
  522.4 19.0 %reduce-scatter.13.cloned.1.call-done = bf16[112,3584]{1,0:T(8,128)(2,1)} async-done(((bf16[896,3584]{1,0:T(8,128)(2,1)}), bf16[112,3584]{1,0:T(8,128)(2,1)}) %reduce-scatter.13.cloned.1.call-update) | async-done | bytes 802832 | tf_op jit(solution)/shard_map/reduce_scatter | solution.py:31
  541.3 42.6 %reduce-scatter.9.cloned.1.call-done = bf16[112,3584]{1,0:T(8,128)(2,1)} async-done(((bf16[896,3584]{1,0:T(8,128)(2,1)}), bf16[112,3584]{1,0:T(8,128)(2,1)}) %reduce-scatter.9.cloned.1.call-update) | async-done | bytes 802832 | tf_op jit(solution)/shard_map/reduce_scatter | solution.py:31
  584.0 42.5 %reduce-scatter.7.cloned.1.call-done = bf16[112,3584]{1,0:T(8,128)(2,1)} async-done(((bf16[896,3584]{1,0:T(8,128)(2,1)}), bf16[112,3584]{1,0:T(8,128)(2,1)}) %reduce-scatter.7.cloned.1.call-update) | async-done | bytes 802832 | tf_op jit(solution)/shard_map/reduce_scatter | solution.py:31
  626.5 22.9 %fusion.9 = bf16[2048,896]{0,1:T(8,128)(2,1)} fusion(bf16[2048,3584]{1,0:T(8,128)(2,1)} %get-tuple-element.29, bf16[1,896,3584]{2,1,0:T(8,128)(2,1)} %all-gather.15.cloned.1.call-done, f32[2048,3584]{1,0:T(8,128)} %fusion.40), kind=kOutput, calls=%fused_computation.19 | convolution fusion | flops 13197377536 | bytes 54132736 | tf_op jit(solution)/shard_map/transpose(jvp())/dot_general | solution.py:22
  649.4 19.7 %fusion.17 = (f32[2048]{0:T(1024)S(1)}, bf16[2048,896]{0,1:T(8,128)(2,1)S(1)}) fusion(bf16[1,2048,896]{1,2,0:T(8,128)(2,1)S(1)} %copy-done, bf16[2048,896]{0,1:T(8,128)(2,1)} %fusion.9, bf16[2048,3584]{1,0:T(8,128)(2,1)} %get-tuple-element.28, bf16[1,896,3584]{2,1,0:T(8,128)(2,1)} %all-gather.13.cloned.1.call-done), kind=kOutput, calls=%fused_computation.39 | convolution fusion | flops 13162510336 | bytes 32120832 | tf_op jit(solution)/shard_map/transpose(jvp())/dot_general | solution.py:21
  679.8 47.1 %all-reduce.3.cloned.1.call-done = (bf16[1,112,3584]{2,1,0:T(8,128)(2,1)}, bf16[1,112,3584]{2,1,0:T(8,128)(2,1)}, bf16[1,112,3584]{2,1,0:T(8,128)(2,1)}, bf16[1,...) async-done(((bf16[1,112,3584]{2,1,0:T(8,128)(2,1)}, bf16[1,112,3584]{2,1,0:T(8,128)(2,1)}, bf16[1,112,3584]{2,1,0:T(8,128)(2,1)}, ...) | async-done | bytes 4816912 | tf_op jit(solution)/shard_map/psum | solution.py:31
  (75 shorter events, 86.8 us)
Async XLA Ops:
  7.2 45.9 %all-gather.13.cloned.1.call-start = ((), (), s32[]{:S(2)}) async-start(), calls=%async_computation.12 | async-start | bytes 7225344 | tf_op jit(solution)/shard_map/all_gather | solution.py:28
  10.1 83.5 %all-gather.15.cloned.1.call-start = ((), (), s32[]{:S(2)}) async-start(), calls=%async_computation.13 | async-start | bytes 7225344 | tf_op jit(solution)/shard_map/all_gather | solution.py:28
  12.8 121.1 %all-gather.17.cloned.1.call-start = ((), (), s32[]{:S(2)}) async-start(), calls=%async_computation.14 | async-start | bytes 7225344 | tf_op jit(solution)/shard_map/all_gather | solution.py:28
  14.3 159.8 %all-gather.21.cloned.1.call-start = ((), (), s32[]{:S(2)}) async-start(), calls=%async_computation.16 | async-start | bytes 7225344 | tf_op jit(solution)/shard_map/all_gather | solution.py:28
  14.9 200.0 %all-gather.23.cloned.1.call-start = ((), (), s32[]{:S(2)}) async-start(), calls=%async_computation.17 | async-start | bytes 7225344 | tf_op jit(solution)/shard_map/all_gather | solution.py:28
  15.6 240.2 %all-gather.19.cloned.1.call-start = ((), (), s32[]{:S(2)}) async-start(), calls=%async_computation.15 | async-start | bytes 7225344 | tf_op jit(solution)/shard_map/all_gather | solution.py:28
  16.2 506.1 %reduce-scatter.15.cloned.1.call-start = ((), (), s32[]{:S(2)}) async-start(), calls=%async_computation.10 | async-start | bytes 7225344 | tf_op jit(solution)/shard_map/reduce_scatter | solution.py:31
  25.8 67.8 %copy-start.8 = (f32[2048]{0:T(1024)}, f32[2048]{0:T(1024)S(1)}, u32[]{:S(2)}) copy-start(f32[2048]{0:T(1024)S(1)} %fusion.61) | copy-start | bytes 24580
  155.0 41.2 %copy-start.12 = (f32[2048]{0:T(1024)}, f32[2048]{0:T(1024)S(1)}, u32[]{:S(2)}) copy-start(f32[2048]{0:T(1024)S(1)} %get-tuple-element.22) | copy-start | bytes 24580
  155.0 186.5 %copy-start.10 = (f32[2048]{0:T(1024)}, f32[2048]{0:T(1024)S(1)}, u32[]{:S(2)}) copy-start(f32[2048]{0:T(1024)S(1)} %fusion.62) | copy-start | bytes 24580
  298.8 22.7 %copy-start.4 = (bf16[2048,896]{0,1:T(8,128)(2,1)S(1)}, bf16[2048,896]{0,1:T(8,128)(2,1)}, u32[]{:S(2)}) copy-start(bf16[2048,896]{0,1:T(8,128)(2,1)} %get-tuple-element.23) | copy-start | bytes 11010052
  321.5 19.9 %copy-start.13 = (f32[2048]{0:T(1024)S(1)}, f32[2048]{0:T(1024)}, u32[]{:S(2)}) copy-start(f32[2048]{0:T(1024)} %copy-done.12) | copy-start | bytes 24580
  321.5 20.0 %copy-start.1 = (bf16[1,2048,896]{1,2,0:T(8,128)(2,1)S(1)}, bf16[1,2048,896]{1,2,0:T(8,128)(2,1)}, u32[]{:S(2)}) copy-start(bf16[1,2048,896]{1,2,0:T(8,128)(2,1)} %copy.9) | copy-start | bytes 11010052
  365.8 156.6 %reduce-scatter.17.cloned.1.call-start = ((), (), s32[]{:S(2)}) async-start(), calls=%async_computation.11 | async-start | bytes 7225344 | tf_op jit(solution)/shard_map/reduce_scatter | solution.py:31
  392.6 129.8 %reduce-scatter.11.cloned.1.call-start = ((), (), s32[]{:S(2)}) async-start(), calls=%async_computation.8 | async-start | bytes 7225344 | tf_op jit(solution)/shard_map/reduce_scatter | solution.py:31
  392.6 42.1 %copy-start.9 = (f32[2048]{0:T(1024)S(1)}, f32[2048]{0:T(1024)}, u32[]{:S(2)}) copy-start(f32[2048]{0:T(1024)} %copy-done.8) | copy-start | bytes 24580
  434.8 24.1 %copy-start.11 = (f32[2048]{0:T(1024)S(1)}, f32[2048]{0:T(1024)}, u32[]{:S(2)}) copy-start(f32[2048]{0:T(1024)} %copy-done.10) | copy-start | bytes 24580
  458.8 82.5 %reduce-scatter.13.cloned.1.call-start = ((), (), s32[]{:S(2)}) async-start(), calls=%async_computation.9 | async-start | bytes 7225344 | tf_op jit(solution)/shard_map/reduce_scatter | solution.py:31
  483.1 100.9 %reduce-scatter.9.cloned.1.call-start = ((), (), s32[]{:S(2)}) async-start(), calls=%async_computation.7 | async-start | bytes 7225344 | tf_op jit(solution)/shard_map/reduce_scatter | solution.py:31
  502.6 123.8 %reduce-scatter.7.cloned.1.call-start = ((), (), s32[]{:S(2)}) async-start(), calls=%async_computation.6 | async-start | bytes 7225344 | tf_op jit(solution)/shard_map/reduce_scatter | solution.py:31
  522.2 204.7 %all-reduce.3.cloned.1.call-start = ((), (), s32[]{:S(2)}) async-start(), calls=%async_computation.18 | async-start | bytes 9633792 | tf_op jit(solution)/shard_map/psum | solution.py:31
  626.5 22.9 %copy-start = (bf16[1,2048,896]{1,2,0:T(8,128)(2,1)S(1)}, bf16[1,2048,896]{1,2,0:T(8,128)(2,1)}, u32[]{:S(2)}) copy-start(bf16[1,2048,896]{1,2,0:T(8,128)(2,1)} %copy.10) | copy-start | bytes 11010052
  649.4 19.8 %copy-start.7 = (f32[2048]{0:T(1024)S(1)}, f32[2048]{0:T(1024)}, u32[]{:S(2)}) copy-start(f32[2048]{0:T(1024)} %copy-done.6) | copy-start | bytes 24580
  649.4 19.8 %copy-start.3 = (bf16[2048,896]{0,1:T(8,128)(2,1)S(1)}, bf16[2048,896]{0,1:T(8,128)(2,1)}, u32[]{:S(2)}) copy-start(bf16[2048,896]{0,1:T(8,128)(2,1)} %copy-done.2) | copy-start | bytes 11010052
  (3 other events, 8.1 us)
Sparse Core Ops, SparseCore 0:
  10.2 42.8 all-gather.12
  54.7 38.7 all-gather.14
  95.1 38.7 all-gather.16
  135.3 38.7 all-gather.20
  176.1 38.7 all-gather.22
  217.0 38.7 all-gather.18
  365.9 39.8 reduce-scatter.14
  408.1 40.2 reduce-scatter.16
  458.9 39.8 reduce-scatter.10
  501.0 40.2 reduce-scatter.12
  543.7 40.2 reduce-scatter.8
  586.1 40.2 reduce-scatter.6
  629.2 97.6 all-reduce.2
where the time goes:
time: 748 us; the launch traced here: 740 us
  matrix products  429 us (57%)
  waiting for transfers between devices  252 us (34%)
  local copies, waits for them, and re-layouts  27.4 us (4%)
  other arithmetic  16.9 us (2%)
  between operations  14.5 us (2%)
    dot_general x6, matrix products, layer(): up = jnp.dot(a, w['w_up'], preferred_element_type=jnp.float32)  152 us
    dot_general x6, matrix products, layer(): gate = jnp.dot(a, w['w_gate'], preferred_element_type=jnp.float32)  146 us
    dot_general x5, matrix products, matmul(): jnp.dot(a, w, preferred_element_type=jnp.float32).astype(jnp.bfloat16)  131 us
    reduce_scatter x6, waiting for transfers between devices, summed(): lax.psum_scatter(term, 's', scatter_dimension=0, tiled=True)  104 us
    all_gather x6, waiting for transfers between devices, fetched(): lax.all_gather(w[number], 's', axis=0, tiled=True)  98.6 us
    psum x1, waiting for transfers between devices, summed(): lax.psum(lax.psum_scatter(term, 's', scatter_dimension=0, tiled=True), 'r')  47.1 us
    unnamed x31, local copies, waits for them, and re-layouts  20.7 us
  transfers between devices with their start and end apart: 13, of which 10 were waited for; matrix products, arithmetic and copies ran while one was open for 48% of the time, Pallas kernels for 0%

commit v1 on v0

v1 whole, which is shorter than its diff:
```python
import functools

import jax
import jax.numpy as jnp
from jax import lax
from jax.experimental import pallas as pl
from jax.experimental.pallas import tpu as pltpu
from jax.sharding import PartitionSpec as P

F32 = jnp.float32
BF16 = jnp.bfloat16
ANY = pl.BlockSpec(memory_space=pl.ANY)
MESH = pl.DeviceIdType.MESH
BLOCK = 512
LANES = 128
VMEM_LIMIT = 67_000_000


def dot(a, b):
    return lax.dot_general(a, b, (((1,), (0,)), ((), ())), preferred_element_type=F32)


def dot_t(a, b):
    return lax.dot_general(a, b, (((1,), (1,)), ((), ())), preferred_element_type=F32)


def rows_of(start, size):
    return pl.ds(pl.multiple_of(start, 16), size)


def lanes_of(start, size):
    return pl.ds(pl.multiple_of(start, LANES), size)


def wait_for(ref, sem):
    pltpu.make_async_copy(ref, ref, sem).wait()


class Place:
    def __init__(self, nr, ns):
        self.nr, self.nx = nr, ns // 2
        self.r, self.s = lax.axis_index("r"), lax.axis_index("s")
        self.x, self.c = self.s // 2, self.s % 2

    def at(self, dx=0, dy=0, dc=0):
        return {"r": (self.r + dy) % self.nr, "s": 2 * ((self.x + dx) % self.nx) + (self.c + dc) % 2}

    def row(self, dx):
        return 2 * ((self.x + dx) % self.nx) + self.c


def send(src, dst, send_sem, recv_sem, device):
    pltpu.make_async_remote_copy(src_ref=src, dst_ref=dst, send_sem=send_sem, recv_sem=recv_sem, device_id=device, device_id_type=MESH).start()


def greet(peers):
    barrier = pltpu.get_barrier_semaphore()
    for peer in peers:
        pl.semaphore_signal(barrier, inc=1, device_id=peer, device_id_type=MESH)
    pl.semaphore_wait(barrier, len(peers))


class Gather:
    def __init__(self, place, nb, shard_rows, down_rows, own, whole, sems):
        self.p, self.nb, self.m, self.dr = place, nb, shard_rows, down_rows
        self.own, self.whole = own, whole
        self.x1s, self.x1r, self.x2s, self.x2r, self.ys, self.yr, self.ds, self.dr_, self.loc = sems
        self.half = place.r % 2
        self.quarter_rows = down_rows // nb // 4

    def piece(self, i):
        n = i % self.nb
        return i // self.nb, 4 * (n % 2) + n // 2, n

    def src(self, i, q, n=1):
        layer, j, t = self.piece(i)
        width = self.nb * LANES
        for k in range(2):
            for e in range(n):
                yield self.own[k].at[layer, :, lanes_of(width * (q + e) + LANES * j, LANES)]
        yield self.own[2].at[layer, rows_of(4 * self.quarter_rows * t + self.quarter_rows * q, n * self.quarter_rows), :]

    def dst(self, i, s, q, n=1, split=False):
        layer, j, t = self.piece(i)
        for k in range(2):
            if split:
                for e in range(n):
                    yield self.whole[k].at[layer, j, rows_of(self.m * s, self.m), lanes_of(LANES * (q + e), LANES)]
            else:
                yield self.whole[k].at[layer, j, rows_of(self.m * s, self.m), lanes_of(LANES * q, n * LANES)]
        yield self.whole[2].at[layer, rows_of(self.dr * s + 4 * self.quarter_rows * t + self.quarter_rows * q, n * self.quarter_rows), :]

    def units(self, a, b, c=1):
        if c == 1:
            return self.whole[0].at[0, 0, : self.m * a, : LANES * b]
        return self.whole[0].at[0, :c, : self.m * a, : LANES * b]

    def first(self, i):
        s = self.p.s
        for d, dx in enumerate((1, -1)):
            for a, b in zip(self.src(i, 2 * self.half, 2), self.dst(i, s, 2 * self.half, 2, True)):
                send(a, b, self.x1s.at[i], self.x1r.at[i, d], self.p.at(dx=dx))
        for a, b in zip(self.src(i, 0, 4), self.dst(i, s, 0, 4, True)):
            send(a, b, self.x1s.at[i], self.dr_.at[i], self.p.at(dc=1))
            pltpu.make_async_copy(a, b, self.loc.at[i]).start()

    def second(self, i):
        for d, dx in enumerate((1, -1)):
            wait_for(self.units(6, 1), self.x1r.at[i, d])
            for a in self.dst(i, self.p.row(-dx), 2 * self.half + d):
                send(a, a, self.x2s.at[i], self.x2r.at[i, d], self.p.at(dx=dx))

    def third(self, i):
        for d in range(2):
            wait_for(self.units(3, 1), self.x2r.at[i, d])
        for d, dy in enumerate((1, -1)):
            for dx in (1, -1, 2):
                for a in self.dst(i, self.p.row(dx), 2 * self.half + d):
                    send(a, a, self.ys.at[i], self.yr.at[i, d], self.p.at(dy=dy))

    def fourth(self, i):
        for d in range(2):
            wait_for(self.units(3, 3), self.yr.at[i, d])
        for dx in (1, -1, 2):
            for a in self.dst(i, self.p.row(dx), 0, 4):
                send(a, a, self.ds.at[i], self.dr_.at[i], self.p.at(dc=1))

    def ready(self, i):
        wait_for(self.units(6, 4, 2), self.dr_.at[i])
        wait_for(self.units(3, 4), self.loc.at[i])

    def sent(self, i):
        wait_for(self.units(6, 4), self.x1s.at[i])
        wait_for(self.units(6, 1), self.x2s.at[i])
        wait_for(self.units(6, 3), self.ys.at[i])
        wait_for(self.units(6, 3, 2), self.ds.at[i])


def normed(h):
    return h * lax.rsqrt(jnp.mean(h * h, -1, keepdims=True) + 1e-6)


def silu(g):
    return g * (jnp.tanh(g * 0.5) * 0.5 + 0.5)


def forward_kernel(nr, ns, x_h, dy_h, og_h, ou_h, od_h, a0_h, xt_h, dyt_h, a1_h, h1t_h, wg_h, wu_h, wd_h, x, a, t1, acc, act, og, ou, od, wg, wu, wd, x1s, x1r, x2s, x2r, ys, yr, ds, dr, loc, io, wsem):
    place = Place(nr, ns)
    tokens, d = x.shape
    nb = wg_h.shape[1]
    pieces = wg_h.shape[0] * nb
    loads = [pltpu.make_async_copy(p, q, io.at[k]) for k, (p, q) in enumerate(((og_h, og), (ou_h, ou), (od_h, od), (x_h, x)))]
    for load in loads:
        load.start()
    greet([place.at(dx=1), place.at(dx=-1), place.at(dy=1), place.at(dy=-1), place.at(dc=1)])
    gather = Gather(place, nb, og.shape[1], od.shape[1], (og, ou, od), (wg_h, wu_h, wd_h), (x1s, x1r, x2s, x2r, ys, yr, ds, dr, loc))
    for load in loads[:3]:
        load.wait()
    gather.first(0)
    loads[3].wait()
    small = 256

    def prepare(k, carry):
        rows = pl.ds(pl.multiple_of(k * small, small), small)
        a[rows, :] = normed(x[rows, :].astype(F32)).astype(BF16)
        t1[:, rows] = x[rows, :].T
        return carry

    lax.fori_loop(0, tokens // small, prepare, 0)
    outs = [pltpu.make_async_copy(a, a0_h, io.at[0]), pltpu.make_async_copy(t1, xt_h, io.at[1])]
    for out in outs:
        out.start()
    acc[...] = jnp.zeros_like(acc)

    def load_up(i, slot):
        _, j, _ = gather.piece(i)
        return [pltpu.make_async_copy(h.at[0, j], v.at[slot], wsem.at[slot, k]) for k, (h, v) in enumerate(((wg_h, wg), (wu_h, wu)))]

    def load_down(i):
        _, j, _ = gather.piece(i)
        return [pltpu.make_async_copy(wd_h.at[0, rows_of(q * nb * LANES + LANES * j, LANES), :], wd.at[pl.ds(q * LANES, LANES), :], wsem.at[2, q]) for q in range(4)]

    big = 1024

    def step(k, carry):
        def stage(run, lag):
            @pl.when((k >= lag) & (k - lag < pieces))
            def _():
                run(k - lag)

        @pl.when((k >= 1) & (k < pieces))
        def _():
            gather.first(k)

        stage(gather.second, 1)
        stage(gather.third, 2)
        stage(gather.fourth, 3)
        stage(gather.ready, 4)

        @pl.when((k >= 4) & (k < 4 + nb))
        def _():
            for load in load_up(k - 4, k % 2):
                load.start()

        @pl.when((k >= 5) & (k < 5 + nb))
        def _():
            i = k - 5
            slot = (k - 1) % 2
            for load in load_down(i):
                load.start()
            for load in load_up(i, slot):
                load.wait()

            def up(n, carry):
                rows = pl.ds(pl.multiple_of(n * big, big), big)
                g = dot(a[rows, :], wg[slot])
                u = dot(a[rows, :], wu[slot])
                act[rows, :] = (silu(g) * u).astype(BF16)
                return carry

            lax.fori_loop(0, tokens // big, up, 0)
            for load in load_down(i):
                load.wait()

            def down(n, carry):
                rows = pl.ds(pl.multiple_of(n * big, big), big)
                acc[rows, :] += dot(act[rows, :], wd[...])
                return carry

            lax.fori_loop(0, tokens // big, down, 0)

        return carry

    lax.fori_loop(0, pieces + 5, step, 0)
    for out in outs:
        out.wait()

    def finish(k, carry):
        rows = pl.ds(pl.multiple_of(k * small, small), small)
        h = (x[rows, :].astype(F32) + acc[rows, :].astype(BF16).astype(F32)).astype(BF16)
        a[rows, :] = normed(h.astype(F32)).astype(BF16)
        t1[:, rows] = h.T
        return carry

    lax.fori_loop(0, tokens // small, finish, 0)
    outs = [pltpu.make_async_copy(a, a1_h, io.at[0]), pltpu.make_async_copy(t1, h1t_h, io.at[1])]
    for out in outs:
        out.start()
    load = pltpu.make_async_copy(dy_h, x, io.at[2])
    load.start()
    for out in outs:
        out.wait()
    load.wait()

    def turn(k, carry):
        rows = pl.ds(pl.multiple_of(k * small, small), small)
        t1[:, rows] = x[rows, :].T
        return carry

    lax.fori_loop(0, tokens // small, turn, 0)
    out = pltpu.make_async_copy(t1, dyt_h, io.at[0])
    out.start()
    out.wait()

    def drain(i, carry):
        gather.sent(i)
        return carry

    lax.fori_loop(0, pieces, drain, 0)


def forward(mesh, x, dy, w_gate, w_up, w_down):
    nr, ns = mesh.shape["r"], mesh.shape["s"]
    tokens, d = x.shape
    layers, m, hidden = w_gate.shape
    nb = hidden // BLOCK
    pieces = layers * nb
    states, turned = jax.ShapeDtypeStruct((tokens, d), BF16), jax.ShapeDtypeStruct((d, tokens), BF16)
    up = jax.ShapeDtypeStruct((layers, nb, d, BLOCK), BF16)
    dma = pltpu.SemaphoreType.DMA
    return pl.pallas_call(
        functools.partial(forward_kernel, nr, ns),
        out_shape=(states, turned, turned, states, turned, up, up, jax.ShapeDtypeStruct((layers, hidden, d), BF16)),
        in_specs=[ANY] * 5,
        out_specs=(ANY,) * 8,
        scratch_shapes=[
            pltpu.VMEM((tokens, d), BF16),
            pltpu.VMEM((tokens, d), BF16),
            pltpu.VMEM((d, tokens), BF16),
            pltpu.VMEM((tokens, d), F32),
            pltpu.VMEM((tokens, BLOCK), BF16),
            pltpu.VMEM(w_gate.shape, BF16),
            pltpu.VMEM(w_up.shape, BF16),
            pltpu.VMEM(w_down.shape, BF16),
            pltpu.VMEM((2, d, BLOCK), BF16),
            pltpu.VMEM((2, d, BLOCK), BF16),
            pltpu.VMEM((BLOCK, d), BF16),
            dma((pieces,)),
            dma((pieces, 2)),
            dma((pieces,)),
            dma((pieces, 2)),
            dma((pieces,)),
            dma((pieces, 2)),
            dma((pieces,)),
            dma((pieces,)),
            dma((pieces,)),
            dma((4,)),
            dma((3, 4)),
        ],
        compiler_params=pltpu.CompilerParams(collective_id=0, has_side_effects=True, vmem_limit_bytes=VMEM_LIMIT),
        name="forward",
    )(x, dy, w_gate, w_up, w_down)


NAMES = ("w_gate", "w_up", "w_down")


def matmul(a, w):
    return jnp.dot(a, w, preferred_element_type=jnp.float32).astype(jnp.bfloat16)


def normed0(h):
    wide = h.astype(jnp.float32)
    scale = lax.rsqrt(jnp.mean(wide**2, -1, keepdims=True) + 1e-6)
    return (wide * scale).astype(jnp.bfloat16)


def layer(h, w):
    a = normed0(h)
    gate = jnp.dot(a, w["w_gate"], preferred_element_type=jnp.float32)
    up = jnp.dot(a, w["w_up"], preferred_element_type=jnp.float32)
    return h + matmul((jax.nn.silu(gate) * up).astype(jnp.bfloat16), w["w_down"])


def solution(mesh):
    def summed(term):
        return lax.psum(lax.psum_scatter(term, "s", scatter_dimension=0, tiled=True), "r")

    def step(x, dy, *weights):
        layers, _, hidden = weights[0].shape
        d = x.shape[-1]
        nb = hidden // BLOCK
        a0, xt, dyt, a1, h1t, wg, wu, wd = forward(mesh, x[0], dy[0], *weights)

        def whole(w):
            return w.reshape(layers, nb, d, 4, LANES).transpose(0, 2, 3, 1, 4).reshape(layers, d, hidden)

        full = (whole(wg), whole(wu), wd)
        inputs = [xt.T, h1t.T]
        by_h, mine = dyt.T, [None] * layers
        for number in reversed(range(layers)):
            w = {name: full[k][number] for k, name in enumerate(NAMES)}
            _, back = jax.vjp(lambda w, h: layer(h, w), w, inputs[number])
            by_w, by_h = back(by_h)
            mine[number] = [summed(by_w[name]) for name in NAMES]
        return (by_h[None], *(jnp.stack([mine[number][i] for number in range(layers)]) for i in range(3)))

    states, cut = P(("rep", "r", "s"), None, None), P(None, "s", None)
    return jax.shard_map(
        step,
        mesh=mesh,
        in_specs=(states, states) + (cut,) * 3,
        out_specs=(states,) + (P("rep", "s", None),) * 3,
        check_vma=False,
    )
```

time: 748 us -> 833 us (1.11)
  waiting for transfers between devices: 252 us -> 117 us
  Pallas kernels: 0 us -> 134 us
  local copies, waits for them, and re-layouts: 27.4 us -> 117 us
  matrix products: 429 us -> 413 us
  other arithmetic: 16.9 us -> 26.8 us
    pallas_call x0 -> x1, Pallas kernels: none -> 134 us  [forward(): pl.pallas_call(functools.partial(forward_kernel, nr, ns), out_shape=(stat...]
    all_gather x6 -> x0, waiting for transfers between devices: 98.6 us -> none  [fetched(): lax.all_gather(w[number], 's', axis=0, tiled=True)]
    reshape x0 -> x4, local copies, waits for them, and re-layouts: none -> 90.9 us  [whole(): w.reshape(layers, nb, d, 4, LANES).transpose(0, 2, 3, 1, 4)]
    reduce_scatter x6, waiting for transfers between devices: 104 us -> 58.2 us  [summed(): lax.psum_scatter(term, 's', scatter_dimension=0, tiled=True)]
    dot_general x5 -> x4, matrix products: 131 us -> 97.3 us  [matmul(): jnp.dot(a, w, preferred_element_type=jnp.float32).astype(jnp.bfloat16)]
    dot_general x6, matrix products: 146 us -> 165 us  [layer(): gate = jnp.dot(a, w['w_gate'], preferred_element_type=jnp.float32)]
    unnamed x31 -> x21, local copies, waits for them, and re-layouts: 20.7 us -> 7.27 us
    slice x3 -> x2, local copies, waits for them, and re-layouts: 6.7 us -> 19.1 us  [step(): w = {name: full[k][number] for k, name in enumerate(NAMES)}]
  transfers between devices with their start and end apart: 13 -> 7, of which waited for: 10 -> 3; matrix products, arithmetic and copies ran while one was open for 48% -> 39% of each run, Pallas kernels for 0% -> 0%
where the time goes in v1:
time: 833 us; the launch traced here: 824 us
  matrix products  413 us (50%)
  Pallas kernels  134 us (16%)
  local copies, waits for them, and re-layouts  117 us (14%)
  waiting for transfers between devices  117 us (14%)
  other arithmetic  26.8 us (3%)
  between operations  14.8 us (2%)
    dot_general x6, matrix products, layer(): gate = jnp.dot(a, w['w_gate'], preferred_element_type=jnp.float32)  165 us
    dot_general x6, matrix products, layer(): up = jnp.dot(a, w['w_up'], preferred_element_type=jnp.float32)  150 us
    pallas_call x1, Pallas kernels, forward(): pl.pallas_call(functools.partial(forward_kernel, nr, ns), out_shape=(stat...  134 us
    dot_general x4, matrix products, matmul(): jnp.dot(a, w, preferred_element_type=jnp.float32).astype(jnp.bfloat16)  97.3 us
    reshape x4, local copies, waits for them, and re-layouts, whole(): w.reshape(layers, nb, d, 4, LANES).transpose(0, 2, 3, 1, 4)  90.9 us
    psum x1, waiting for transfers between devices, summed(): lax.psum(lax.psum_scatter(term, 's', scatter_dimension=0, tiled=True), 'r')  58.8 us
    reduce_scatter x6, waiting for transfers between devices, summed(): lax.psum_scatter(term, 's', scatter_dimension=0, tiled=True)  58.2 us
    slice x2, local copies, waits for them, and re-layouts, step(): w = {name: full[k][number] for k, name in enumerate(NAMES)}  19.1 us
  transfers between devices with their start and end apart: 7, of which 3 were waited for; matrix products, arithmetic and copies ran while one was open for 39% of the time, Pallas kernels for 0%

profile of v1, /device:TPU:97, one launch (start us, length us, event | category | flops | bytes accessed | tf_op | source)
XLA Modules:
  0.0 823.5 jit_solution(6915396022977794962)
XLA Ops:
  7.2 134.2 %forward.1 = (bf16[2048,896]{1,0:T(8,128)(2,1)}, bf16[896,2048]{1,0:T(8,128)(2,1)}, bf16[896,2048]{1,0:T(8,128)(2,1)}, bf16[2048,896]{1,0:T(8,128)(2,1)}, bf16[8...) custom-call(bf16[2048,896]{1,0:T(8,128)(2,1)} %bitcast.94, ...), custom_call_target="tpu_custom_call" | custom-call | tf_op jit(solution)/shard_map/forward/pallas_call | solution.py:281
  141.5 22.5 %reshape.56 = bf16[2,7,896,4,128]{4,3,2,1,0:T(4,128)(2,1)} reshape(bf16[2,7,896,512]{3,2,1,0:T(8,128)(2,1)} %get-tuple-element.12) | data formatting | bytes 25690112 | tf_op jit(solution)/shard_map/reshape | solution.py:346
  164.0 22.9 %copy.10 = bf16[2,7,896,4,128]{2,4,1,3,0:T(8,128)(2,1)} copy(bf16[2,7,896,4,128]{4,3,2,1,0:T(4,128)(2,1)} %reshape.56) | data formatting | bytes 25690112 | tf_op jit(solution)/shard_map/reshape | solution.py:346
  197.9 22.5 %reshape.57 = bf16[2,7,896,4,128]{4,3,2,1,0:T(4,128)(2,1)} reshape(bf16[2,7,896,512]{3,2,1,0:T(8,128)(2,1)} %get-tuple-element.14) | data formatting | bytes 25690112 | tf_op jit(solution)/shard_map/reshape | solution.py:346
  220.5 22.9 %copy.11 = bf16[2,7,896,4,128]{2,4,1,3,0:T(8,128)(2,1)} copy(bf16[2,7,896,4,128]{4,3,2,1,0:T(4,128)(2,1)} %reshape.57) | data formatting | bytes 25690112 | tf_op jit(solution)/shard_map/reshape | solution.py:346
  252.9 22.2 %convolution_convert_fusion.1 = bf16[2048,3584]{1,0:T(8,128)(2,1)} fusion(bf16[896,2048]{1,0:T(8,128)(2,1)} %get-tuple-element.10, bf16[2,3584,896]{2,1,0:T(8,128)(2,1)} %get-tuple-element.13), kind=kOutput, calls=%fused_computation.21 | convolution fusion | flops 13160677376 | bytes 24772608 | tf_op jit(solution)/shard_map/transpose(jvp())/dot_general | solution.py:319
  275.1 24.4 %fusion.35 = f32[2048,3584]{1,0:T(8,128)} fusion(bf16[896,3584]{0,1:T(8,128)(2,1)} %bitcast.92, bf16[896,2048]{1,0:T(8,128)(2,1)} %get-tuple-element.11, f32[2048]{0:T(1024)S(1)} %fusion.45), kind=kOutput, calls=%fused_computation.59 | convolution fusion | flops 13158842368 | bytes 39460864 | tf_op jit(solution)/shard_map/jvp()/dot_general | solution.py:331
  299.5 42.7 %fusion.1 = (bf16[2048,3584]{1,0:T(8,128)(2,1)}, f32[2048,3584]{1,0:T(8,128)}) fusion(f32[2048,3584]{1,0:T(8,128)} %fusion.35, bf16[2048,3584]{1,0:T(8,128)(2,1)} %convolution_convert_fusion.1, bf16[896,3584]{0,1:T(8,128)(2,1)} %bitcast.90, bf16[896,2048]{1,0:T(8,128)(2,1)} %get-tuple-element.11, f32[2048]{0:T(1024)S(1)} %fusion.45), kind=kOutput, calls=%fused_computation.7 | convolution fusion | flops 13246922752 | bytes 98181120 | tf_op jit(solution)/shard_map/jvp()/dot_general | solution.py:330
  342.2 23.9 %fusion.25 = bf16[896,3584]{1,0:T(8,128)(2,1)} fusion(bf16[2048,3584]{1,0:T(8,128)(2,1)} %convolution_convert_fusion.1, bf16[896,2048]{1,0:T(8,128)(2,1)} %get-tuple-element.11, f32[2048]{0:T(1024)S(1)} %fusion.45, f32[2048,3584]{1,0:T(8,128)} %get-tuple-element.35), kind=kOutput, calls=%fused_computation.47 | convolution fusion | flops 13206093824 | bytes 54140928 | tf_op jit(solution)/shard_map/transpose(jvp())/dot_general | solution.py:331
  366.3 20.0 %convolution_convert_fusion.2 = bf16[896,3584]{1,0:T(8,128)(2,1)} fusion(bf16[2048,3584]{1,0:T(8,128)(2,1)} %get-tuple-element.34, bf16[896,2048]{1,0:T(8,128)(2,1)} %get-tuple-element.11, f32[2048]{0:T(1024)S(1)} %fusion.45), kind=kOutput, calls=%fused_computation.48 | convolution fusion | flops 13158842368 | bytes 24780800 | tf_op jit(solution)/shard_map/transpose(jvp())/dot_general | solution.py:330
  386.4 26.6 %fusion.22 = bf16[3584,896]{1,0:T(8,128)(2,1)} fusion(bf16[896,2048]{1,0:T(8,128)(2,1)} %get-tuple-element.10, f32[2048,3584]{1,0:T(8,128)} %fusion.35, f32[2048,3584]{1,0:T(8,128)} %get-tuple-element.35), kind=kOutput, calls=%fused_computation.44 | convolution fusion | flops 13200588800 | bytes 68812800 | tf_op jit(solution)/shard_map/transpose(jvp())/dot_general | solution.py:319
  413.1 20.1 %fusion.55 = bf16[2048,896]{0,1:T(8,128)(2,1)} fusion(bf16[2048,3584]{1,0:T(8,128)(2,1)} %get-tuple-element.34, bf16[896,3584]{0,1:T(8,128)(2,1)} %bitcast.91), kind=kOutput, calls=%fused_computation.74 | convolution fusion | flops 13153337344 | bytes 24772608 | tf_op jit(solution)/shard_map/transpose(jvp())/dot_general | solution.py:330
  436.6 26.3 %fusion.14 = (f32[2048]{0:T(1024)S(1)}, bf16[2048,896]{0,1:T(8,128)(2,1)}) fusion(bf16[896,2048]{1,0:T(8,128)(2,1)} %get-tuple-element.11, bf16[2048,896]{0,1:T(8,128)(2,1)} %fusion.55, bf16[896,3584]{0,1:T(8,128)(2,1)} %bitcast.93, bf16[2048,3584]{1,0:T(8,128)(2,1)} %convolution_convert_fusion.1, f32[2048,3584]{1,0:T(8,128)} %get-tuple-element.35), kind=kOutput, calls=%fused_computation.30 | convolution fusion | flops 13208385536 | bytes 61480960 | tf_op jit(solution)/shard_map/transpose(jvp())/dot_general | solution.py:331
  463.0 24.8 %fusion.41 = f32[2048,3584]{1,0:T(8,128)} fusion(bf16[896,3584]{0,1:T(8,128)(2,1)} %bitcast.86, bf16[896,2048]{1,0:T(8,128)(2,1)} %get-tuple-element.15, f32[2048]{0:T(1024)S(1)} %fusion.46), kind=kOutput, calls=%fused_computation.61 | convolution fusion | flops 13158842368 | bytes 39460864 | tf_op jit(solution)/shard_map/jvp()/dot_general | solution.py:331
  495.5 22.0 %convolution_convert_fusion = bf16[2048,3584]{1,0:T(8,128)(2,1)} fusion(bf16[2048,896]{0,1:T(8,128)(2,1)} %fusion.32, bf16[2,3584,896]{2,1,0:T(8,128)(2,1)} %get-tuple-element.13), kind=kOutput, calls=%fused_computation.20 | convolution fusion | flops 13160677376 | bytes 24772608 | tf_op jit(solution)/shard_map/transpose(jvp())/dot_general | solution.py:319
  517.5 42.7 %fusion.3 = (bf16[2048,3584]{1,0:T(8,128)(2,1)}, f32[2048,3584]{1,0:T(8,128)}) fusion(f32[2048,3584]{1,0:T(8,128)} %fusion.41, bf16[2048,3584]{1,0:T(8,128)(2,1)} %convolution_convert_fusion, bf16[896,3584]{0,1:T(8,128)(2,1)} %bitcast.88, bf16[896,2048]{1,0:T(8,128)(2,1)} %get-tuple-element.15, f32[2048]{0:T(1024)S(1)} %fusion.46), kind=kOutput, calls=%fused_computation.9 | convolution fusion | flops 13246922752 | bytes 98181120 | tf_op jit(solution)/shard_map/jvp()/dot_general | solution.py:330
  560.2 23.9 %fusion.24 = bf16[896,3584]{1,0:T(8,128)(2,1)} fusion(bf16[2048,3584]{1,0:T(8,128)(2,1)} %convolution_convert_fusion, bf16[896,2048]{1,0:T(8,128)(2,1)} %get-tuple-element.15, f32[2048]{0:T(1024)S(1)} %fusion.46, f32[2048,3584]{1,0:T(8,128)} %get-tuple-element.39), kind=kOutput, calls=%fused_computation.46 | convolution fusion | flops 13206093824 | bytes 54140928 | tf_op jit(solution)/shard_map/transpose(jvp())/dot_general | solution.py:331
  584.2 19.7 %convolution_convert_fusion.3 = bf16[896,3584]{1,0:T(8,128)(2,1)} fusion(bf16[2048,3584]{1,0:T(8,128)(2,1)} %get-tuple-element.38, bf16[896,2048]{1,0:T(8,128)(2,1)} %get-tuple-element.15, f32[2048]{0:T(1024)S(1)} %fusion.46), kind=kOutput, calls=%fused_computation.49 | convolution fusion | flops 13158842368 | bytes 24780800 | tf_op jit(solution)/shard_map/transpose(jvp())/dot_general | solution.py:330
  604.0 26.5 %fusion.23 = bf16[3584,896]{1,0:T(8,128)(2,1)} fusion(bf16[2048,896]{0,1:T(8,128)(2,1)} %fusion.32, f32[2048,3584]{1,0:T(8,128)} %fusion.41, f32[2048,3584]{1,0:T(8,128)} %get-tuple-element.39), kind=kOutput, calls=%fused_computation.45 | convolution fusion | flops 13200588800 | bytes 68812800 | tf_op jit(solution)/shard_map/transpose(jvp())/dot_general | solution.py:319
  630.7 20.2 %fusion.56 = bf16[2048,896]{0,1:T(8,128)(2,1)} fusion(bf16[2048,3584]{1,0:T(8,128)(2,1)} %get-tuple-element.38, bf16[896,3584]{0,1:T(8,128)(2,1)} %bitcast.89), kind=kOutput, calls=%fused_computation.75 | convolution fusion | flops 13153337344 | bytes 24772608 | tf_op jit(solution)/shard_map/transpose(jvp())/dot_general | solution.py:330
  651.0 15.7 %reduce-scatter.7.cloned.1.call-done = bf16[112,3584]{1,0:T(8,128)(2,1)} async-done(((bf16[896,3584]{1,0:T(8,128)(2,1)}), bf16[112,3584]{1,0:T(8,128)(2,1)}) %reduce-scatter.7.cloned.1.call-update) | async-done | bytes 802832 | tf_op jit(solution)/shard_map/reduce_scatter | solution.py:337
  666.7 42.5 %reduce-scatter.15.cloned.1.call-done = bf16[448,896]{1,0:T(8,128)(2,1)} async-done(((bf16[3584,896]{1,0:T(8,128)(2,1)}), bf16[448,896]{1,0:T(8,128)(2,1)}) %reduce-scatter.15.cloned.1.call-update) | async-done | bytes 802832 | tf_op jit(solution)/shard_map/reduce_scatter | solution.py:337
  709.2 26.5 %fusion.17 = (f32[2048]{0:T(1024)S(1)}, bf16[2048,896]{0,1:T(8,128)(2,1)}) fusion(bf16[896,2048]{1,0:T(8,128)(2,1)} %get-tuple-element.15, bf16[2048,896]{0,1:T(8,128)(2,1)} %fusion.56, bf16[896,3584]{0,1:T(8,128)(2,1)} %bitcast.87, bf16[2048,3584]{1,0:T(8,128)(2,1)} %convolution_convert_fusion, f32[2048,3584]{1,0:T(8,128)} %get-tuple-element.39), kind=kOutput, calls=%fused_computation.33 | convolution fusion | flops 13208385536 | bytes 61480960 | tf_op jit(solution)/shard_map/transpose(jvp())/dot_general | solution.py:331
  750.8 58.8 %all-reduce.3.cloned.1.call-done = (bf16[1,112,3584]{2,1,0:T(8,128)(2,1)}, bf16[1,112,3584]{2,1,0:T(8,128)(2,1)}, bf16[1,112,3584]{2,1,0:T(8,128)(2,1)}, bf16[1,...) async-done(((bf16[1,112,3584]{2,1,0:T(8,128)(2,1)}, bf16[1,112,3584]{2,1,0:T(8,128)(2,1)}, bf16[1,112,3584]{2,1,0:T(8,128)(2,1)}, ...) | async-done | bytes 4816912 | tf_op jit(solution)/shard_map/psum | solution.py:337
  (51 shorter events, 54.1 us)
Async XLA Ops:
  7.2 643.8 %reduce-scatter.13.cloned.1.call-start = ((), (), s32[]{:S(2)}) async-start(), calls=%async_computation.9 | async-start | bytes 7225344 | tf_op jit(solution)/shard_map/reduce_scatter | solution.py:337
  186.9 9.6 %copy-start = (bf16[896,2048]{1,0:T(8,128)(2,1)S(1)}, bf16[896,2048]{1,0:T(8,128)(2,1)}, u32[]{:S(2)}) copy-start(bf16[896,2048]{1,0:T(8,128)(2,1)} %get-tuple-element.11) | copy-start | bytes 11010052
  197.3 0.6 copy-start.4
  197.9 168.4 %copy-start.8 = (f32[2048]{0:T(1024)}, f32[2048]{0:T(1024)S(1)}, u32[]{:S(2)}) copy-start(f32[2048]{0:T(1024)S(1)} %fusion.45) | copy-start | bytes 24580
  366.2 284.7 %reduce-scatter.9.cloned.1.call-start = ((), (), s32[]{:S(2)}) async-start(), calls=%async_computation.7 | async-start | bytes 7225344 | tf_op jit(solution)/shard_map/reduce_scatter | solution.py:337
  386.3 264.6 %reduce-scatter.17.cloned.1.call-start = ((), (), s32[]{:S(2)}) async-start(), calls=%async_computation.11 | async-start | bytes 7225344 | tf_op jit(solution)/shard_map/reduce_scatter | solution.py:337
  413.1 237.9 %reduce-scatter.11.cloned.1.call-start = ((), (), s32[]{:S(2)}) async-start(), calls=%async_computation.8 | async-start | bytes 7225344 | tf_op jit(solution)/shard_map/reduce_scatter | solution.py:337
  436.0 0.6 copy-start.2
  436.6 147.6 %copy-start.6 = (f32[2048]{0:T(1024)}, f32[2048]{0:T(1024)S(1)}, u32[]{:S(2)}) copy-start(f32[2048]{0:T(1024)S(1)} %fusion.46) | copy-start | bytes 24580
  436.6 26.3 %copy-start.5 = (f32[2048]{0:T(1024)S(1)}, f32[2048]{0:T(1024)}, u32[]{:S(2)}) copy-start(f32[2048]{0:T(1024)} %copy-done.4) | copy-start | bytes 24580
  463.0 24.8 %copy-start.1 = (bf16[896,2048]{1,0:T(8,128)(2,1)S(1)}, bf16[896,2048]{1,0:T(8,128)(2,1)}, u32[]{:S(2)}) copy-start(bf16[896,2048]{1,0:T(8,128)(2,1)} %get-tuple-element.11) | copy-start | bytes 11010052
  463.0 24.8 %copy-start.9 = (f32[2048]{0:T(1024)S(1)}, f32[2048]{0:T(1024)}, u32[]{:S(2)}) copy-start(f32[2048]{0:T(1024)} %copy-done.8) | copy-start | bytes 24580
  584.1 82.6 %reduce-scatter.7.cloned.1.call-start = ((), (), s32[]{:S(2)}) async-start(), calls=%async_computation.6 | async-start | bytes 7225344 | tf_op jit(solution)/shard_map/reduce_scatter | solution.py:337
  603.9 105.2 %reduce-scatter.15.cloned.1.call-start = ((), (), s32[]{:S(2)}) async-start(), calls=%async_computation.10 | async-start | bytes 7225344 | tf_op jit(solution)/shard_map/reduce_scatter | solution.py:337
  630.6 179.0 %all-reduce.3.cloned.1.call-start = ((), (), s32[]{:S(2)}) async-start(), calls=%async_computation.12 | async-start | bytes 9633792 | tf_op jit(solution)/shard_map/psum | solution.py:337
  709.2 26.5 %copy-start.3 = (f32[2048]{0:T(1024)S(1)}, f32[2048]{0:T(1024)}, u32[]{:S(2)}) copy-start(f32[2048]{0:T(1024)} %copy-done.2) | copy-start | bytes 24580
  709.2 26.6 %copy-start.7 = (f32[2048]{0:T(1024)S(1)}, f32[2048]{0:T(1024)}, u32[]{:S(2)}) copy-start(f32[2048]{0:T(1024)} %copy-done.6) | copy-start | bytes 24580
Sparse Core Ops, SparseCore 0:
  366.3 39.9 reduce-scatter.12
  408.7 40.2 reduce-scatter.8
  451.3 40.2 reduce-scatter.16
  584.2 39.9 reduce-scatter.10
  626.4 40.2 reduce-scatter.6
  668.9 40.2 reduce-scatter.14
  711.9 97.6 all-reduce.2

commit v2 on v1

--- a/solution.py
+++ b/solution.py
@@ -312,48 +312,351 @@
     )(x, dy, w_gate, w_up, w_down)
 
 
-NAMES = ("w_gate", "w_up", "w_down")
-
-
-def matmul(a, w):
-    return jnp.dot(a, w, preferred_element_type=jnp.float32).astype(jnp.bfloat16)
-
-
-def normed0(h):
-    wide = h.astype(jnp.float32)
-    scale = lax.rsqrt(jnp.mean(wide**2, -1, keepdims=True) + 1e-6)
-    return (wide * scale).astype(jnp.bfloat16)
-
-
-def layer(h, w):
-    a = normed0(h)
-    gate = jnp.dot(a, w["w_gate"], preferred_element_type=jnp.float32)
-    up = jnp.dot(a, w["w_up"], preferred_element_type=jnp.float32)
-    return h + matmul((jax.nn.silu(gate) * up).astype(jnp.bfloat16), w["w_down"])
+class Reduce:
+    def __init__(self, place, nb, layers, terms, pair, hop1, hop2, side, final, outs, sems):
+        self.p, self.nb, self.layers = place, nb, layers
+        self.tg, self.td = terms
+        self.pg, self.pd = pair
+        self.h1g, self.h1d = hop1
+        self.h2g, self.h2d = hop2
+        self.sg, self.sd = side
+        self.fg, self.fd = final
+        self.og, self.ou, self.od = outs
+        self.ps, self.pr, self.h1s, self.h1r, self.h2s, self.h2r, self.ss, self.sr, self.fs, self.fl, self.fx, self.rg, self.rd = sems
+        self.m = self.pg.shape[3]
+
+    def own_rows(self, x, c):
+        return rows_of(self.m * (2 * x + c), self.m)
+
+    def down_rows(self, x, c):
+        return rows_of(128 * x + 64 * c, 64)
+
+    def at_x(self, dx):
+        return (self.p.x + dx) % self.p.nx
+
+    def units(self, a, b):
+        return self.tg.at[0, 0, : self.m * a, : LANES * b]
+
+    def pair_gate(self, b, k):
+        slot, other = b % 3, 1 - self.p.c
+        for x in range(self.p.nx):
+            send(self.tg.at[slot, k, self.own_rows(x, other), :], self.pg.at[slot, x, k], self.ps.at[slot], self.pr.at[slot], self.p.at(dc=1))
+
+    def pair_down(self, b):
+        slot, other = b % 3, 1 - self.p.c
+        for x in range(self.p.nx):
+            send(self.td.at[slot, self.down_rows(x, other), :], self.pd.at[slot, x], self.ps.at[slot], self.pr.at[slot], self.p.at(dc=1))
+
+    def both(self, slot, x, k, cols=None):
+        cols = slice(None) if cols is None else cols
+        return self.tg[slot, k, self.own_rows(x, self.p.c), cols].astype(F32) + self.pg[slot, x, k, :, cols].astype(F32)
+
+    def both_down(self, slot, x, start=0, size=64):
+        mine = self.td[slot, rows_of(128 * x + 64 * self.p.c + start, size), :].astype(F32)
+        return mine + self.pd[slot, x, pl.ds(start, size), :].astype(F32)
+
+    def first(self, b):
+        slot, two = b % 3, b % 2
+        wait_for(self.tg.at[0, :, : self.m * 6, :], self.ps.at[slot])
+        wait_for(self.tg.at[0, :, : self.m * 6, :], self.pr.at[slot])
+        x = self.at_x(2)
+        for k in range(2):
+            self.pg[slot, x, k] = self.both(slot, x, k).astype(BF16)
+        self.pd[slot, x] = self.both_down(slot, x).astype(BF16)
+        for d, dx in enumerate((1, -1)):
+            for k in range(2):
+                send(self.pg.at[slot, x, k, :, pl.ds(256 * d, 256)], self.h1g.at[two, d, k], self.h1s.at[two], self.h1r.at[two, d], self.p.at(dx=dx))
+            send(self.pd.at[slot, x, pl.ds(32 * d, 32), :], self.h1d.at[two, d], self.h1s.at[two], self.h1r.at[two, d], self.p.at(dx=dx))
+
+    def second(self, b):
+        slot, two = b % 3, b % 2
+        wait_for(self.units(6, 2), self.h1s.at[two])
+        for d in range(2):
+            wait_for(self.units(6, 1), self.h1r.at[two, d])
+        for d, dx in enumerate((1, -1)):
+            x = self.at_x(dx)
+            with_hop, alone = slice(256 * d, 256 * d + 256), slice(256 - 256 * d, 512 - 256 * d)
+            for k in range(2):
+                self.pg[slot, x, k, :, with_hop] = (self.both(slot, x, k, with_hop) + self.h1g[two, d, k].astype(F32)).astype(BF16)
+                self.pg[slot, x, k, :, alone] = self.both(slot, x, k, alone).astype(BF16)
+            self.pd[slot, x, pl.ds(32 * d, 32), :] = (self.both_down(slot, x, 32 * d, 32) + self.h1d[two, d].astype(F32)).astype(BF16)
+            self.pd[slot, x, pl.ds(32 - 32 * d, 32), :] = self.both_down(slot, x, 32 - 32 * d, 32).astype(BF16)
+            for k in range(2):
+                send(self.pg.at[slot, x, k], self.h2g.at[two, d, k], self.h2s.at[two], self.h2r.at[two, d], self.p.at(dx=dx))
+            send(self.pd.at[slot, x], self.h2d.at[two, d], self.h2s.at[two], self.h2r.at[two, d], self.p.at(dx=dx))
+
+    def chip_sum(self, b, k, q):
+        slot, two = b % 3, b % 2
+        cols = lanes_of(LANES * q, LANES)
+        return self.both(slot, self.p.x, k, cols) + self.h2g[two, 0, k, :, cols].astype(F32) + self.h2g[two, 1, k, :, cols].astype(F32)
+
+    def chip_sum_down(self, b, q):
+        slot, two = b % 3, b % 2
+        rows = rows_of(16 * q, 16)
+        mine = self.td[slot, rows_of(128 * self.p.x + 64 * self.p.c + 16 * q, 16), :].astype(F32) + self.pd[slot, self.p.x, rows, :].astype(F32)
+        return mine + self.h2d[two, 0, rows, :].astype(F32) + self.h2d[two, 1, rows, :].astype(F32)
+
+    def third(self, b):
+        slot, two = b % 3, b % 2
+        wait_for(self.units(6, 4), self.h2s.at[two])
+        for d in range(2):
+            wait_for(self.units(3, 4), self.h2r.at[two, d])
+        for dy in range(1, self.p.nr):
+            q = (self.p.r + dy) % self.p.nr
+            cols, rows = lanes_of(LANES * q, LANES), rows_of(16 * q, 16)
+            for k in range(2):
+                self.pg[slot, self.p.x, k, :, cols] = self.chip_sum(b, k, q).astype(BF16)
+            self.pd[slot, self.p.x, rows, :] = self.chip_sum_down(b, q).astype(BF16)
+            for k in range(2):
+                send(self.pg.at[slot, self.p.x, k, :, cols], self.sg.at[two, dy - 1, k], self.ss.at[two], self.sr.at[two, dy - 1], self.p.at(dy=dy))
+            send(self.pd.at[slot, self.p.x, rows, :], self.sd.at[two, dy - 1], self.ss.at[two], self.sr.at[two, dy - 1], self.p.at(dy=dy))
+
+    def fourth(self, b):
+        two = b % 2
+        layer, j = self.layers - 1 - b // self.nb, b % self.nb
+        wait_for(self.units(3, 3), self.ss.at[two])
+        for n in range(self.p.nr - 1):
+            wait_for(self.units(3, 1), self.sr.at[two, n])
+
+        @pl.when(b >= 2)
+        def _():
+            self.final_sent(two)
+
+        q = self.p.r
+        for k in range(2):
+            total = self.chip_sum(b, k, q)
+            for n in range(self.p.nr - 1):
+                total += self.sg[two, n, k].astype(F32)
+            self.fg[two, k] = total.astype(BF16)
+        total = self.chip_sum_down(b, q)
+        for n in range(self.p.nr - 1):
+            total += self.sd[two, n].astype(F32)
+        self.fd[two] = total.astype(BF16)
+
+        cols = lanes_of(self.nb * LANES * q + LANES * j, LANES)
+        share = self.od.shape[1]
+        place = 128 * j + 64 * self.p.c
+        owner = place // share
+        rows = rows_of(place + 16 * q - share * owner, 16)
+        for dy in range(1, self.p.nr):
+            for k, out in enumerate((self.og, self.ou)):
+                send(self.fg.at[two, k], out.at[layer, :, cols], self.fs.at[two], self.rg.at[0], self.p.at(dy=dy))
+            peer = {"r": (self.p.r + dy) % self.p.nr, "s": 2 * self.p.x + owner}
+            send(self.fd.at[two], self.od.at[layer, rows, :], self.fs.at[two], self.rd.at[0], peer)
+        for k, out in enumerate((self.og, self.ou)):
+            pltpu.make_async_copy(self.fg.at[two, k], out.at[layer, :, cols], self.fl.at[two]).start()
+
+        @pl.when(owner == self.p.c)
+        def _():
+            pltpu.make_async_copy(self.fd.at[two], self.od.at[layer, rows, :], self.fx.at[two]).start()
+
+        @pl.when(owner != self.p.c)
+        def _():
+            send(self.fd.at[two], self.od.at[layer, rows, :], self.fx.at[two], self.rd.at[0], self.p.at(dc=1))
+
+    def final_sent(self, two):
+        wait_for(self.units(3, 3), self.fs.at[two])
+        wait_for(self.units(2, 1), self.fl.at[two])
+        wait_for(self.units(1, 1), self.fx.at[two])
+
+
+def gates(g, u, d):
+    sig = jnp.tanh(g * 0.5) * 0.5 + 0.5
+    s = g * sig
+    d = d.astype(BF16).astype(F32)
+    return (s * u).astype(BF16), (d * u * (sig + s - s * sig)).astype(BF16), (d * s).astype(BF16)
+
+
+def backward_kernel(
+    nr, ns, dy_h, dyt_h, a0_h, xt_h, a1_h, h1t_h, wg_h, wu_h, wd_h, dx_h, gg_h, gu_h, gd_h,
+    a, at, dy, dyt, ht, dat, act, dg, du, wg, wu, wd, tg, td, pg, pd, h1g, h1d, h2g, h2d, sg, sd, fg, fd,
+    ps, pr, h1s, h1r, h2s, h2r, ss, sr, fs, fl, fx, rg, rd, io, wsem,
+):
+    place = Place(nr, ns)
+    tokens, d = a.shape
+    layers, nb = wg_h.shape[:2]
+    steps = layers * nb
+    loads = [pltpu.make_async_copy(p, q, io.at[k]) for k, (p, q) in enumerate(((h1t_h, at), (a1_h, a), (dy_h, dy), (dyt_h, dyt), (h1t_h, ht)))]
+    for load in loads:
+        load.start()
+
+    def weights(b, slot):
+        layer, j = layers - 1 - b // nb, b % nb
+        yield pltpu.make_async_copy(wg_h.at[layer, j], wg.at[slot], wsem.at[slot, 0])
+        yield pltpu.make_async_copy(wu_h.at[layer, j], wu.at[slot], wsem.at[slot, 1])
+        for q in range(4):
+            yield pltpu.make_async_copy(wd_h.at[layer, rows_of(q * nb * LANES + LANES * j, LANES), :], wd.at[slot, pl.ds(q * LANES, LANES), :], wsem.at[slot, 2 + q])
+
+    for load in weights(0, 0):
+        load.start()
+    peers = [place.at(dx=1), place.at(dx=-1), place.at(dc=1)]
+    for dy_ in range(1, nr):
+        peers += [place.at(dy=dy_), place.at(dy=dy_, dc=1)]
+    greet(peers)
+    reduce = Reduce(
+        place, nb, layers, (tg, td), (pg, pd), (h1g, h1d), (h2g, h2d), (sg, sd), (fg, fd), (gg_h, gu_h, gd_h),
+        (ps, pr, h1s, h1r, h2s, h2r, ss, sr, fs, fl, fx, rg, rd),
+    )
+    small, big = 256, 1024
+
+    def norm_turned():
+        def chunk(n, carry):
+            cols = pl.ds(pl.multiple_of(n * small, small), small)
+            h = at[:, cols].astype(F32)
+            at[:, cols] = (h * lax.rsqrt(jnp.mean(h * h, 0, keepdims=True) + 1e-6)).astype(BF16)
+            return carry
+
+        lax.fori_loop(0, tokens // small, chunk, 0)
+
+    loads[0].wait()
+    norm_turned()
+    dat[...] = jnp.zeros_like(dat)
+    for load in loads[1:]:
+        load.wait()
+
+    def layer_end(last):
+        def chunk(n, carry):
+            cols = pl.ds(pl.multiple_of(n * small, small), small)
+            h = ht[:, cols].astype(F32)
+            scale = lax.rsqrt(jnp.mean(h * h, 0, keepdims=True) + 1e-6)
+            h = h * scale
+            da = dat[:, cols].astype(BF16).astype(F32)
+            v = dyt[:, cols].astype(F32) + scale * (da - h * jnp.mean(da * h, 0, keepdims=True))
+            v = v.astype(BF16)
+            if not last:
+                dyt[:, cols] = v
+                dat[:, cols] = jnp.zeros((d, small), F32)
+            dy[cols, :] = v.T
+            return carry
+
+        lax.fori_loop(0, tokens // small, chunk, 0)
+
+    def compute(k):
+        slot = k % 2
+        for load in weights(k, slot):
+            load.wait()
+
+        @pl.when(k + 1 < steps)
+        def _():
+            for load in weights(k + 1, 1 - slot):
+                load.start()
+
+        def chunk(n, carry):
+            rows = pl.ds(pl.multiple_of(n * big, big), big)
+            g = dot(a[rows, :], wg[slot])
+            u = dot(a[rows, :], wu[slot])
+            e = dot_t(dy[rows, :], wd[slot])
+            act[rows, :], dg[rows, :], du[rows, :] = gates(g, u, e)
+            return carry
+
+        lax.fori_loop(0, tokens // big, chunk, 0)
+
+    def terms(k):
+        slot = k % 3
+        for n, left in enumerate((dg, du)):
+            for e in range(BLOCK // 256):
+                cols = slice(256 * e, 256 * e + 256)
+                tg[slot, n, :, cols] = dot(at[...], left[:, cols]).astype(BF16)
+            reduce.pair_gate(k, n)
+        for e in range(BLOCK // 256):
+            cols = slice(256 * e, 256 * e + 256)
+            td[slot, cols, :] = dot(dyt[...], act[:, cols]).astype(BF16).T
+        reduce.pair_down(k)
+
+    def back(k):
+        slot = k % 2
+
+        def chunk(n, carry):
+            cols = pl.ds(pl.multiple_of(n * big, big), big)
+            dat[:, cols] += dot_t(wg[slot], dg[cols, :]) + dot_t(wu[slot], du[cols, :])
+            return carry
+
+        lax.fori_loop(0, tokens // big, chunk, 0)
+
+    def step(k, carry):
+        def stage(run, lag):
+            @pl.when((k >= lag) & (k - lag < steps))
+            def _():
+                run(k - lag)
+
+        stage(reduce.third, 2)
+        stage(reduce.first, 1)
+        stage(compute, 0)
+
+        @pl.when(k == steps)
+        def _():
+            pltpu.make_async_copy(xt_h, ht, io.at[4]).wait()
+            layer_end(True)
+            pltpu.make_async_copy(dy, dx_h, io.at[0]).start()
+
+        stage(reduce.second, 1)
+        stage(reduce.fourth, 2)
+        stage(terms, 0)
+        stage(back, 0)
+
+        @pl.when(k == nb - 1)
+        def _():
+            loads = [pltpu.make_async_copy(p, q, io.at[n]) for n, (p, q) in enumerate(((a0_h, a), (xt_h, at)))]
+            for load in loads:
+                load.start()
+            layer_end(False)
+            pltpu.make_async_copy(xt_h, ht, io.at[4]).start()
+            for load in loads:
+                load.wait()
+            norm_turned()
+
+        return carry
+
+    lax.fori_loop(0, steps + 2, step, 0)
+    reduce.final_sent(0)
+    reduce.final_sent(1)
+    wait_for(wg_h.at[0, :3, : 7 * place_rows(gg_h), :], rg.at[0])
+    wait_for(wg_h.at[0, :2, : 6 * place_rows(gg_h), :], rd.at[0])
+    pltpu.make_async_copy(dy, dx_h, io.at[0]).wait()
+
+
+def place_rows(ref):
+    return ref.shape[1]
+
+
+def backward(mesh, dy, dyt, a0, xt, a1, h1t, wg, wu, wd):
+    nr, ns = mesh.shape["r"], mesh.shape["s"]
+    nx = ns // 2
+    tokens, d = dy.shape
+    layers, nb = wg.shape[:2]
+    hidden = nb * BLOCK
+    m, share = d // ns, hidden // ns
+    dma = pltpu.SemaphoreType.DMA
+    vmem = lambda *shape, dtype=BF16: pltpu.VMEM(shape, dtype)
+    up = jax.ShapeDtypeStruct((layers, m, hidden), BF16)
+    return pl.pallas_call(
+        functools.partial(backward_kernel, nr, ns),
+        out_shape=(jax.ShapeDtypeStruct((tokens, d), BF16), up, up, jax.ShapeDtypeStruct((layers, share, d), BF16)),
+        in_specs=[ANY] * 9,
+        out_specs=(ANY,) * 4,
+        scratch_shapes=[
+            vmem(tokens, d), vmem(d, tokens), vmem(tokens, d), vmem(d, tokens), vmem(d, tokens), vmem(d, tokens, dtype=F32),
+            vmem(tokens, BLOCK), vmem(tokens, BLOCK), vmem(tokens, BLOCK),
+            vmem(2, d, BLOCK), vmem(2, d, BLOCK), vmem(2, BLOCK, d),
+            vmem(3, 2, d, BLOCK), vmem(3, BLOCK, d),
+            vmem(3, nx, 2, m, BLOCK), vmem(3, nx, 64, d),
+            vmem(2, 2, 2, m, BLOCK // 2), vmem(2, 2, 32, d),
+            vmem(2, 2, 2, m, BLOCK), vmem(2, 2, 64, d),
+            vmem(2, nr - 1, 2, m, LANES), vmem(2, nr - 1, 16, d),
+            vmem(2, 2, m, LANES), vmem(2, 16, d),
+            dma((3,)), dma((3,)), dma((2,)), dma((2, 2)), dma((2,)), dma((2, 2)), dma((2,)), dma((2, 3)), dma((2,)), dma((2,)), dma((2,)),
+            dma((1,)), dma((1,)), dma((5,)), dma((2, 6)),
+        ],
+        compiler_params=pltpu.CompilerParams(collective_id=1, has_side_effects=True, vmem_limit_bytes=VMEM_LIMIT),
+        name="backward",
+    )(dy, dyt, a0, xt, a1, h1t, wg, wu, wd)
 
 
 def solution(mesh):
-    def summed(term):
-        return lax.psum(lax.psum_scatter(term, "s", scatter_dimension=0, tiled=True), "r")
-
     def step(x, dy, *weights):
-        layers, _, hidden = weights[0].shape
-        d = x.shape[-1]
-        nb = hidden // BLOCK
         a0, xt, dyt, a1, h1t, wg, wu, wd = forward(mesh, x[0], dy[0], *weights)
-
-        def whole(w):
-            return w.reshape(layers, nb, d, 4, LANES).transpose(0, 2, 3, 1, 4).reshape(layers, d, hidden)
-
-        full = (whole(wg), whole(wu), wd)
-        inputs = [xt.T, h1t.T]
-        by_h, mine = dyt.T, [None] * layers
-        for number in reversed(range(layers)):
-            w = {name: full[k][number] for k, name in enumerate(NAMES)}
-            _, back = jax.vjp(lambda w, h: layer(h, w), w, inputs[number])
-            by_w, by_h = back(by_h)
-            mine[number] = [summed(by_w[name]) for name in NAMES]
-        return (by_h[None], *(jnp.stack([mine[number][i] for number in range(layers)]) for i in range(3)))
+        dx, gg, gu, gd = backward(mesh, dy[0], dyt, a0, xt, a1, h1t, wg, wu, wd)
+        return dx[None], gg, gu, gd
 
     states, cut = P(("rep", "r", "s"), None, None), P(None, "s", None)
     return jax.shard_map(

time: 833 us -> 455 us (0.55); the launches traced: 824 us -> 454 us
  matrix products: 413 us -> 0 us
  Pallas kernels: 134 us -> 446 us
  waiting for transfers between devices: 117 us -> 0 us
  local copies, waits for them, and re-layouts: 117 us -> 7.79 us
  other arithmetic: 26.8 us -> 0 us
  between operations: 14.8 us -> 0.67 us
    dot_general x16 -> x0, matrix products: 413 us -> none  [the longest x6 165 us: layer(): gate = jnp.dot(a, w['w_gate'], preferred_element_type=jnp.float32)]
    pallas_call x0 -> x1, Pallas kernels: none -> 312 us  [backward(): pl.pallas_call(functools.partial(backward_kernel, nr, ns), out_shape=(jax...]
    reshape x4 -> x0, local copies, waits for them, and re-layouts: 90.9 us -> none  [whole(): w.reshape(layers, nb, d, 4, LANES).transpose(0, 2, 3, 1, 4)]
    psum x1 -> x0, waiting for transfers between devices: 58.8 us -> none  [summed(): lax.psum(lax.psum_scatter(term, 's', scatter_dimension=0, tiled=True), 'r')]
    reduce_scatter x6 -> x0, waiting for transfers between devices: 58.2 us -> none  [summed(): lax.psum_scatter(term, 's', scatter_dimension=0, tiled=True)]
    slice x2 -> x0, local copies, waits for them, and re-layouts: 19.1 us -> none  [step(): w = {name: full[k][number] for k, name in enumerate(NAMES)}]
    broadcast_in_dim x1 -> x0, other arithmetic: 9.01 us -> none  [step(): by_h[None]]
  transfers between devices with their start and end apart: 7 -> 0, of which waited for: 3 -> 0; matrix products, arithmetic and copies ran while one was open for 39% -> 0% of each run, Pallas kernels for 0% -> 0%
where the time goes in v2:
time: 455 us; the launch traced here: 454 us
  Pallas kernels  446 us (98%)
  local copies, waits for them, and re-layouts  7.79 us (2%)
    pallas_call x1, Pallas kernels, backward(): pl.pallas_call(functools.partial(backward_kernel, nr, ns), out_shape=(jax...  312 us
    pallas_call x1, Pallas kernels, forward(): pl.pallas_call(functools.partial(forward_kernel, nr, ns), out_shape=(stat...  134 us

profile of v2, /device:TPU:97, one launch (start us, length us, event | category | flops | bytes accessed | tf_op | source)
XLA Modules:
  0.0 454.4 jit_solution(15403905351744482096)
XLA Ops:
  0.6 134.2 %forward.1 = (bf16[2048,896]{1,0:T(8,128)(2,1)}, bf16[896,2048]{1,0:T(8,128)(2,1)}, bf16[896,2048]{1,0:T(8,128)(2,1)}, bf16[2048,896]{1,0:T(8,128)(2,1)}, bf16[8...) custom-call(bf16[2048,896]{1,0:T(8,128)(2,1)} %bitcast.6, ...), custom_call_target="tpu_custom_call" | custom-call | tf_op jit(solution)/shard_map/forward/pallas_call | solution.py:281
  134.9 311.7 %backward.1 = (bf16[2048,896]{1,0:T(8,128)(2,1)}, bf16[2,112,3584]{2,1,0:T(8,128)(2,1)}, bf16[2,112,3584]{2,1,0:T(8,128)(2,1)}, bf16[2,448,896]{2,1,0:T(8,128)(2,1)}) custom-call(bf16[2048,896]{1,0:T(8,128)(2,1)} %bitcast.4, bf16[896,2048]{1,0:T(8,128)(2,1)} %get-tuple-element.16.dyt_h, bf16[2048,896]{1,0:T(8,128)(2,1)} %get-tuple-element.17.a0_h, ...), custom_call_target="tpu_custom_call" | custom-call | tf_op jit(solution)/shard_map/backward/pallas_call | solution.py:632
  446.6 0.0 copy-start.2
  446.6 0.0 copy-start.1
  446.6 4.3 copy.13
  450.9 0.0 copy-done.2
  450.9 0.0 copy-start
  450.9 1.2 copy.14
  452.1 0.0 copy-done.1
  452.1 1.2 copy.15
  453.2 0.0 copy-done
  453.2 1.2 copy.16
Async XLA Ops:
  446.6 4.3 copy-start.2
  446.6 5.5 %copy-start.1 = (bf16[2,112,3584]{2,1,0:T(8,128)(2,1)S(1)}, bf16[2,112,3584]{2,1,0:T(8,128)(2,1)}, u32[]{:S(2)}) copy-start(bf16[2,112,3584]{2,1,0:T(8,128)(2,1)} %get-tuple-element.34) | copy-start | bytes 4816900
  450.9 2.3 copy-start

commit v3 on v0

v3 whole, which is shorter than its diff:
```python
import functools

import jax
import jax.numpy as jnp
from jax import lax
from jax.experimental import pallas as pl
from jax.experimental.pallas import tpu as pltpu
from jax.sharding import PartitionSpec as P

F32 = jnp.float32
BF16 = jnp.bfloat16
ANY = pl.BlockSpec(memory_space=pl.ANY)
MESH = pl.DeviceIdType.MESH
BLOCK = 512
LANES = 128
VMEM_LIMIT = 67_000_000
HOPS = (1, -1)
CORES = PAIR = range(2)
QUARTERS = 4
SMALL, BIG = 256, 1024
ALL = slice(None)
COLUMNS = [slice(n, n + SMALL) for n in range(0, BLOCK, SMALL)]
PARTS = [slice(n, n + BLOCK) for n in range(0, BIG, BLOCK)]


def dot(a, b):
    return lax.dot_general(a, b, (((1,), (0,)), ((), ())), preferred_element_type=F32)


def dot_t(a, b):
    return lax.dot_general(a, b, (((1,), (1,)), ((), ())), preferred_element_type=F32)


def rows_of(start, size):
    return pl.ds(pl.multiple_of(start, 16), size)


def lanes_of(start, size):
    return pl.ds(pl.multiple_of(start, LANES), size)


def wait_for(ref, sem):
    pltpu.make_async_copy(ref, ref, sem).wait()


class Place:
    def __init__(self, nr, ns):
        self.nr, self.nx = nr, ns // 2
        self.r, self.s = lax.axis_index("r"), lax.axis_index("s")
        self.x, self.c = self.s // 2, self.s % 2

    def at(self, dx=0, dy=0, dc=0):
        return {"r": (self.r + dy) % self.nr, "s": 2 * ((self.x + dx) % self.nx) + (self.c + dc) % 2}

    def row(self, dx):
        return 2 * ((self.x + dx) % self.nx) + self.c


def odd(n):
    return n % 2


def slot3(n):
    return n % 3


def units(ref, m, n):
    for blocks in (1, 2, 3):
        for lanes in (QUARTERS, 3, 1):
            rows, left = divmod(n, blocks * lanes)
            if not left and rows * m <= ref.shape[1]:
                return ref.at[:blocks, : m * rows, : LANES * lanes]
    raise ValueError(n)


def copies(pairs, sems):
    return [pltpu.make_async_copy(a, b, sems.at[n]) for n, (a, b) in enumerate(pairs)]


def start(things):
    for thing in things:
        thing.start()


def wait(things):
    for thing in things:
        thing.wait()


def send(src, dst, send_sem, recv_sem, device):
    pltpu.make_async_remote_copy(src_ref=src, dst_ref=dst, send_sem=send_sem, recv_sem=recv_sem, device_id=device, device_id_type=MESH).start()


def greet(peers):
    barrier = pltpu.get_barrier_semaphore()
    for peer in peers:
        pl.semaphore_signal(barrier, inc=1, device_id=peer, device_id_type=MESH)
    pl.semaphore_wait(barrier, len(peers))


class Gather:
    def __init__(self, place, whole, shard_rows, down_rows, sems):
        self.p, self.m, self.dr = place, shard_rows, down_rows
        self.up, self.down = whole
        self.nb = self.up.shape[1]
        self.x1s, self.x1r, self.x2s, self.x2r, self.ys, self.yr, self.ds, self.dr_, self.loc = sems
        self.half = place.r % 2
        self.qr = down_rows // self.nb // QUARTERS

    def piece(self, i):
        n = i % self.nb
        return i // self.nb, 4 * (odd(n)) + n // 2, n

    def rows(self, n, s, q):
        return self.qr * (QUARTERS * ((n + odd(s)) % self.nb) + q)

    def src(self, own, i, q, n):
        layer, j, t = self.piece(i)
        width = self.nb * LANES
        for e in range(n):
            yield own[0].at[layer, :, :, lanes_of(width * (q + e) + LANES * j, LANES)]
        yield own[1].at[layer, rows_of(self.rows(t, self.p.s, q), n * self.qr), :]

    def dst(self, i, s, q, n, split=False):
        layer, j, t = self.piece(i)
        rows = rows_of(self.m * s, self.m)
        if split:
            for e in range(n):
                yield self.up.at[layer, j, :, rows, lanes_of(LANES * (q + e), LANES)]
        else:
            yield self.up.at[layer, j, :, rows, lanes_of(LANES * q, n * LANES)]
        yield self.down.at[layer, rows_of(self.dr * s + self.rows(t, s, q), n * self.qr), :]

    def units(self, n):
        return units(self.up.at[0, :, 0], self.m, n)

    def own(self, own, i):
        for a, b in zip(self.src(own, i, 0, QUARTERS), self.dst(i, self.p.s, 0, QUARTERS, True)):
            send(a, b, self.x1s.at[i], self.dr_.at[i], self.p.at(dc=1))
            pltpu.make_async_copy(a, b, self.loc.at[i]).start()

    def first(self, i, own=None):
        for d, dx in enumerate(HOPS):
            there = list(self.dst(i, self.p.s, 2 * self.half, 2, own is not None))
            here = there if own is None else self.src(own, i, 2 * self.half, 2)
            for a, b in zip(here, there):
                send(a, b, self.x1s.at[i], self.x1r.at[i, d], self.p.at(dx=dx))

    def second(self, i):
        for d, dx in enumerate(HOPS):
            wait_for(self.units(6), self.x1r.at[i, d])
            for a in self.dst(i, self.p.row(-dx), 2 * self.half + d, 1):
                send(a, a, self.x2s.at[i], self.x2r.at[i, d], self.p.at(dx=dx))
        self.along(i, HOPS)

    def along(self, i, hops):
        for dx in hops:
            for d, dy in enumerate(HOPS):
                for a in self.dst(i, self.p.row(dx), 2 * self.half + d, 1):
                    send(a, a, self.ys.at[i], self.yr.at[i, d], self.p.at(dy=dy))

    def across(self, i, q, n):
        for dx in (*HOPS, 2):
            for a in self.dst(i, self.p.row(dx), q, n):
                send(a, a, self.ds.at[i], self.dr_.at[i], self.p.at(dc=1))

    def third(self, i, early=False):
        for d in PAIR:
            wait_for(self.units(3), self.x2r.at[i, d])
        self.along(i, (2,))
        if early:
            self.across(i, 2 * self.half, 2)

    def fourth(self, i, early=False):
        for d in PAIR:
            wait_for(self.units(9), self.yr.at[i, d])
        if early:
            self.across(i, 2 - 2 * self.half, 2)
        else:
            self.across(i, 0, QUARTERS)

    def sent(self, i, x1):
        for n, sem in ((x1, self.x1s), (6, self.x2s), (18, self.ys), (36, self.ds)):
            wait_for(self.units(n), sem.at[i])


def gate(g):
    sig = jnp.tanh(g * 0.5) * 0.5 + 0.5
    return sig, g * sig


def normed(h):
    return h * lax.rsqrt(jnp.mean(h * h, -1, keepdims=True) + 1e-6)


AHEAD = 2


def forward_kernel(
    nr, ns, x_h, dy_h, og_h, ou_h, od_h, xt_h, dyt_h, a0t_h, a1_h, a1t_h, h1t_h, wup_h, wd_h, f_h, act_h,
    x, y, a, t1, t2, t3, acc, act, f, oup, od, wup, wd, x1s, x1r, x2s, x2r, ys, yr, ds, dr, loc, io, wsem, fsem, asem,
):
    place = Place(nr, ns)
    tokens, d = x.shape
    layers, nb = wup_h.shape[:2]
    pieces, every = nb + AHEAD, layers * nb
    shards = lambda n: [(h.at[n], v) for h, v in ((og_h, oup.at[n, 0]), (ou_h, oup.at[n, 1]), (od_h, od.at[n]))]
    loads = shards(0) + [(x_h, x), (dy_h, y)] + shards(1)
    loads = copies(loads, io)
    start(loads)
    greet([place.at(dc=1)] + [place.at(**{dim: hop}) for dim in ("dx", "dy") for hop in HOPS])
    own = (oup, od)
    gather = Gather(place, (wup_h, wd_h), oup.shape[2], od.shape[1], (x1s, x1r, x2s, x2r, ys, yr, ds, dr, loc))

    def prepare(k, carry):
        rows = rows_of(k * SMALL, SMALL)
        h = x[rows, :]
        n = normed(h.astype(F32)).astype(BF16)
        a[rows, :] = n
        t3[:, rows] = n.T
        t1[:, rows] = h.T
        return carry

    def turn(k, carry):
        rows = rows_of(k * SMALL, SMALL)
        t2[:, rows] = y[rows, :].T
        return carry

    def begin(i):
        gather.first(i, own)
        gather.own(own, i)

    wait(loads[:3])
    begin(0)
    gather.own(own, 1)
    wait(loads[3:4])
    lax.fori_loop(0, tokens // SMALL, prepare, 0)
    gather.second(0)
    for i in (1, 2):
        gather.first(i, own)
    wait(loads[4:5])
    lax.fori_loop(0, tokens // SMALL, turn, 0)
    acc[...] = jnp.zeros_like(acc)
    wait(loads[5:])
    with jax.named_scope("third"):
        gather.third(0, True)
        gather.second(1)
        gather.first(3, own)
        gather.own(own, 2)
        gather.own(own, 3)
    outs = copies(((t1, xt_h), (t2, dyt_h), (t3, a0t_h)), io)
    with jax.named_scope("fourth"):
        gather.fourth(0, True)
    with jax.named_scope("more"):
        gather.third(1)
        gather.second(2)

    def load_up(i):
        _, j, _ = gather.piece(i)
        return pltpu.make_async_copy(wup_h.at[0, j], wup.at[odd(i)], wsem.at[odd(i), 0])

    def load_down(i):
        _, j, _ = gather.piece(i)
        return copies([(wd_h.at[0, rows_of((q * nb + j) * LANES, LANES), :], wd.at[odd(i), pl.ds(q * LANES, LANES), :]) for q in range(QUARTERS)], wsem.at[2 + odd(i)])


    def keep(i, n):
        return [pltpu.make_async_copy(f.at[n, e], f_h.at[e, i, rows_of(n * BIG, BIG), :], fsem.at[n, e]) for e in PAIR]

    def keep_act(i):
        return pltpu.make_async_copy(act.at[odd(i)], act_h.at[i], asem.at[odd(i)])

    def up(i, between):
        slot = odd(i)
        load_up(i).wait()

        @pl.when(i >= 1)
        def _():
            start((*keep(i - 1, 1), keep_act(i - 1)))

        @pl.when(i >= 2)
        def _():
            keep_act(i - 2).wait()

        def chunk(n, carry):
            @pl.when(i >= 1)
            def _():
                wait(keep(i - 1, n))

            for part in PARTS:
                rows, here = rows_of(n * BIG + part.start, BLOCK), slice(part.start, part.stop)
                for cols in COLUMNS:
                    g = dot(a[rows, :], wup[slot, 0, :, cols])
                    u = dot(a[rows, :], wup[slot, 1, :, cols])
                    sig, s = gate(g)
                    act[slot, rows, cols] = (s * u).astype(BF16)
                    f[n, 0, here, cols] = s
                    f[n, 1, here, cols] = u * (sig + s - s * sig)

            @pl.when(n == 0)
            def _():
                start(keep(i, n))
                between()

            return carry

        lax.fori_loop(0, tokens // BIG, chunk, 0)

    def down(i):
        wait(load_down(i))

        def chunk(n, carry):
            rows = rows_of(n * BIG, BIG)
            acc[rows, :] += dot(act[odd(i), rows, :], wd[odd(i)])
            return carry

        lax.fori_loop(0, tokens // BIG, chunk, 0)

    def ready(i):
        wait_for(gather.units(48), dr.at[i])
        wait_for(gather.units(12), loc.at[i])

    with jax.named_scope("ready"):
        ready(0)
    load_up(0).start()
    last = pieces - 2

    def step(i, carry):
        def between():
            with jax.named_scope("gather"):
                for n, run in enumerate((gather.fourth, gather.third, gather.second, begin), 1):

                    @pl.when(i + n <= last)
                    def _():
                        run(i + n)

                    @pl.when(i + n == last)
                    def _():
                        run(last + 1)

                @pl.when(pieces + i < every)
                def _():
                    gather.own(own, pieces + i)

        with jax.named_scope("up"):
            up(i, between)

        @pl.when(i + 1 < nb)
        def _():
            with jax.named_scope("ready"):
                ready(i + 1)
            load_up(i + 1).start()

        start(load_down(i))
        for n, out in enumerate(outs, 2):

            @pl.when(i == n)
            def _(out=out):
                out.start()

        @pl.when(i >= 1)
        def _():
            with jax.named_scope("down"):
                down(i - 1)

        return carry

    lax.fori_loop(0, nb, step, 0)
    wait((*outs, *load_down(nb - 1)))
    start((*keep(nb - 1, 1), keep_act(nb - 1)))
    finals = ((a, a1_h, 0), (t3, a1t_h, 1), (t1, h1t_h, 1))

    def finish(k, carry):
        for e in PAIR:
            rows = rows_of((2 * k + e) * SMALL, SMALL)
            y = acc[rows, :] + dot(act[(nb - 1) % 2, rows, :], wd[(nb - 1) % 2])
            h = (x[rows, :].astype(F32) + y.astype(BF16).astype(F32)).astype(BF16)
            n = normed(h.astype(F32)).astype(BF16)
            a[rows, :] = n
            t3[:, rows] = n.T
            t1[:, rows] = h.T
        rows = rows_of(2 * k * SMALL, 2 * SMALL)
        for n, (p, q, dim) in enumerate(finals):
            part = (ALL,) * dim + (rows,)
            pltpu.make_async_copy(p.at[part], q.at[part], io.at[n]).start()
        return carry

    with jax.named_scope("finish"):
        lax.fori_loop(0, tokens // SMALL // 2, finish, 0)
    for i in range(nb, pieces):
        ready(i)

    def drain(i, carry):
        gather.sent(i, 24)
        return carry

    lax.fori_loop(0, pieces, drain, 0)

    def drain_own(i, carry):
        for sem in (x1s, dr, loc):
            wait_for(gather.units(12), sem.at[i])
        return carry

    lax.fori_loop(pieces, every, drain_own, 0)
    for n in PAIR:
        wait((*keep(nb - 1, n), keep_act(nb - 1 - n)))
    wait(copies([pair[:2] for pair in finals], io))


def array(*shape, dtype=BF16):
    return jax.ShapeDtypeStruct(shape, dtype)


def vmem(*shape, dtype=BF16):
    return pltpu.VMEM(shape, dtype)


def sems(*shapes):
    return [pltpu.SemaphoreType.DMA(shape if isinstance(shape, tuple) else (shape,)) for shape in shapes]


def gather_sems(n):
    return sems(n, (n, 2), n, (n, 2), n, (n, 2), n, n, n)


def call(kernel, mesh, name, ident, outs, scratch, args, aliases={}):
    return pl.pallas_call(
        functools.partial(kernel, mesh.shape["r"], mesh.shape["s"]),
        out_shape=outs,
        in_specs=[ANY] * len(args),
        out_specs=(ANY,) * len(outs),
        input_output_aliases=aliases,
        scratch_shapes=scratch,
        compiler_params=pltpu.CompilerParams(collective_id=ident, has_side_effects=ident is not None, vmem_limit_bytes=VMEM_LIMIT),
        name=name,
    )(*args)


def forward(mesh, x, dy, w_gate, w_up, w_down):
    tokens, d = x.shape
    layers, m, hidden = w_gate.shape
    nb = hidden // BLOCK
    states, turned = array(tokens, d), array(d, tokens)
    outs = (turned, turned, turned, states, turned, turned, array(layers, nb, 2, d, BLOCK), array(layers, hidden, d), array(2, nb, tokens, BLOCK, dtype=F32), array(nb, tokens, BLOCK))
    scratch = [
        *[vmem(tokens, d)] * 3, *[vmem(d, tokens)] * 3, vmem(tokens, d, dtype=F32), vmem(2, tokens, BLOCK), vmem(2, 2, BIG, BLOCK, dtype=F32),
        vmem(layers, 2, m, hidden), vmem(*w_down.shape), vmem(2, 2, d, BLOCK), vmem(2, BLOCK, d),
        *gather_sems(layers * nb), *sems(8, (QUARTERS, QUARTERS), (2, 2), 2),
    ]
    return call(forward_kernel, mesh, "forward", 0, outs, scratch, (x, dy, w_gate, w_up, w_down))


class Reduce:
    def __init__(self, place, like, nb, layers, bufs, outs, sems):
        self.p, self.like, self.nb, self.layers = place, like, nb, layers
        self.tu, self.td, self.pu, self.pd, self.h1u, self.h1d, self.h2u, self.h2d, self.su, self.sd, self.fu, self.fd = bufs
        self.out_up, self.out_down = outs
        self.ps, self.pr, self.h1s, self.h1r, self.h2s, self.h2r, self.ss, self.sr, self.fs, self.fl, self.fx, self.ru, self.rd = sems
        self.m, self.rows = self.pu.shape[3], self.pd.shape[2]

    def own_rows(self, x, c):
        return rows_of(self.m * (2 * x + c), self.m)

    def down_rows(self, x, c):
        return rows_of(self.rows * (2 * x + c), self.rows)

    def at_x(self, dx):
        return (self.p.x + dx) % self.p.nx

    def wait(self, n, sem):
        wait_for(units(self.like, self.m, n), sem)

    def pair_up(self, b, k):
        slot, other = slot3(b), 1 - self.p.c
        for x in range(self.p.nx):
            send(self.tu.at[slot, k, self.own_rows(x, other), :], self.pu.at[slot, x, k], self.ps.at[slot], self.pr.at[slot], self.p.at(dc=1))

    def pair_down(self, b):
        slot, other = slot3(b), 1 - self.p.c
        for x in range(self.p.nx):
            send(self.td.at[slot, self.down_rows(x, other), :], self.pd.at[slot, x], self.ps.at[slot], self.pr.at[slot], self.p.at(dc=1))

    def cut(self, n, parts):
        return lanes_of(BLOCK // parts * n, BLOCK // parts), rows_of(self.rows // parts * n, self.rows // parts)

    def both(self, b, x, n, parts):
        slot = slot3(b)
        cols, rows = self.cut(n, parts)
        mine = rows_of(self.rows * (2 * x + self.p.c) + self.rows // parts * n, self.rows // parts)
        up = self.tu[slot, :, self.own_rows(x, self.p.c), cols].astype(F32) + self.pu[slot, x, :, :, cols].astype(F32)
        return up, self.td[slot, mine, :].astype(F32) + self.pd[slot, x, rows, :].astype(F32)

    def ship(self, b, x, n, parts, sums, to, send_sem, recv_sem, device):
        slot = slot3(b)
        cols, rows = self.cut(n, parts)
        refs = self.pu.at[slot, x, :, :, cols], self.pd.at[slot, x, rows, :]
        for ref, value in zip(refs, sums):
            ref[...] = value.astype(BF16)
        for ref, there in zip(refs, to):
            send(ref, there, send_sem, recv_sem, device)

    def hop(self, b, d, n, sums):
        slot = slot3(b)
        cols, rows = self.cut(n, 2)
        to = self.h2u.at[slot, d, :, :, cols], self.h2d.at[slot, d, rows, :]
        self.ship(b, self.at_x(HOPS[d]), n, 2, sums, to, self.h2s.at[slot], self.h2r.at[slot, d], self.p.at(dx=HOPS[d]))

    def first(self, b):
        slot, two = slot3(b), odd(b)
        self.wait(48, self.ps.at[slot])
        self.wait(48, self.pr.at[slot])
        x = self.at_x(2)
        for d, dx in enumerate(HOPS):
            to = self.h1u.at[two, d], self.h1d.at[two, d]
            self.ship(b, x, d, 2, self.both(b, x, d, 2), to, self.h1s.at[two], self.h1r.at[two, d], self.p.at(dx=dx))
        for d, dx in enumerate(HOPS):
            self.hop(b, d, 1 - d, self.both(b, self.at_x(dx), 1 - d, 2))

    def second(self, b):
        two = odd(b)
        for d in PAIR:
            self.wait(6, self.h1r.at[two, d])
        for d, dx in enumerate(HOPS):
            up, down = self.both(b, self.at_x(dx), d, 2)
            self.hop(b, d, d, (up + self.h1u[two, d].astype(F32), down + self.h1d[two, d].astype(F32)))

    def chip_sum(self, b, q):
        slot = slot3(b)
        cols, rows = self.cut(q, QUARTERS)
        up, down = self.both(b, self.p.x, q, QUARTERS)
        for d in PAIR:
            up, down = up + self.h2u[slot, d, :, :, cols].astype(F32), down + self.h2d[slot, d, rows, :].astype(F32)
        return up, down

    def third(self, b):
        slot, two = slot3(b), odd(b)
        self.wait(12, self.h1s.at[two])
        self.wait(24, self.h2s.at[slot])
        for d in PAIR:
            self.wait(12, self.h2r.at[slot, d])
        for n in range(self.p.nr - 1):
            q = (self.p.r + n + 1) % self.p.nr
            to = self.su.at[two, n], self.sd.at[two, n]
            self.ship(b, self.p.x, q, QUARTERS, self.chip_sum(b, q), to, self.ss.at[two], self.sr.at[two, n], self.p.at(dy=n + 1))

    def fourth(self, b):
        two = odd(b)
        layer, n = self.layers - 1 - b // self.nb, b % self.nb
        j = 4 * (odd(n)) + n // 2
        self.wait(9, self.ss.at[two])
        for n in range(self.p.nr - 1):
            self.wait(3, self.sr.at[two, n])

        @pl.when(b >= 2)
        def _():
            self.final_sent(two)

        q = self.p.r
        up, down = self.chip_sum(b, q)
        for n in range(self.p.nr - 1):
            up, down = up + self.su[two, n].astype(F32), down + self.sd[two, n].astype(F32)
        self.fu[two] = up.astype(BF16)
        self.fd[two] = down.astype(BF16)

        up_to = self.out_up.at[:, layer, :, lanes_of(LANES * (self.nb * q + j), LANES)]
        share = self.out_down.shape[1]
        first = self.rows * (2 * j + self.p.c)
        owner = first // share
        quarter = self.rows // QUARTERS
        down_to = self.out_down.at[layer, rows_of(first + quarter * q - share * owner, quarter), :]
        for dy in range(1, self.p.nr):
            send(self.fu.at[two], up_to, self.fs.at[two], self.ru.at[0], self.p.at(dy=dy))
            peer = {"r": (self.p.r + dy) % self.p.nr, "s": 2 * self.p.x + owner}
            send(self.fd.at[two], down_to, self.fs.at[two], self.rd.at[0], peer)
        pltpu.make_async_copy(self.fu.at[two], up_to, self.fl.at[two]).start()

        @pl.when(owner == self.p.c)
        def _():
            pltpu.make_async_copy(self.fd.at[two], down_to, self.fx.at[two]).start()

        @pl.when(owner != self.p.c)
        def _():
            send(self.fd.at[two], down_to, self.fx.at[two], self.rd.at[0], self.p.at(dc=1))

    def final_sent(self, two):
        for n, sem in ((9, self.fs), (2, self.fl), (1, self.fx)):
            self.wait(n, sem.at[two])


def backward_kernel(
    nr, ns, dy_h, dyt_h, a0t_h, xt_h, a1_h, a1t_h, h1t_h, f_h, act_h, wup_in, wd_in, dx_h, gup_h, gd_h, wup_h, wd_h, kept_h,
    a, at, dy, dyt, ht, dat, f, act, dg, du, wup, wd, tu, td, pu, pd, h1u, h1d, h2u, h2d, su, sd, fu, fd,
    ps, pr, h1s, h1r, h2s, h2r, ss, sr, fs, fl, fx, ru, rd, x1s, x1r, x2s, x2r, ys, yr, ds, dr, _, io, wsem, ksem, fsem,
):
    place = Place(nr, ns)
    tokens, d = a.shape
    layers, nb = wup_h.shape[:2]
    steps = layers * nb
    loads = copies(((a1_h, a), (dy_h, dy), (a1t_h, at), (dyt_h, dyt), (h1t_h, ht)), io)
    gather = Gather(place, (wup_h, wd_h), gup_h.shape[2], gd_h.shape[1], (x1s, x1r, x2s, x2r, ys, yr, ds, dr, None))
    ahead = nb + AHEAD

    def block_of(b):
        return gather.piece(steps - nb + b % nb - (b // nb) * nb)

    def load_up(b):
        layer, j, _ = block_of(b)
        return pltpu.make_async_copy(wup_h.at[layer, j], wup.at[odd(b)], wsem.at[odd(b), 0])

    def load_down(b):
        layer, j, _ = block_of(b)
        return copies([(wd_h.at[layer, rows_of((q * nb + j) * LANES, LANES), :], wd.at[odd(b), pl.ds(q * LANES, LANES), :]) for q in range(QUARTERS)], wsem.at[2 + odd(b)])

    start((*loads[:2], load_up(0), *load_down(0)))
    greet([place.at(dc=1)] + [place.at(dx=hop) for hop in HOPS] + [place.at(dy=hop, dc=c) for hop in range(1, nr) for c in CORES])
    reduce = Reduce(
        place, wup_h.at[0, :, 0], nb, layers, (tu, td, pu, pd, h1u, h1d, h2u, h2d, su, sd, fu, fd), (gup_h, gd_h),
        (ps, pr, h1s, h1r, h2s, h2r, ss, sr, fs, fl, fx, ru, rd),
    )
    dat[...] = jnp.zeros_like(dat)
    wait(loads[:2])
    start(loads[2:])

    def layer_end(begin, end, last):
        def chunk(n, carry):
            cols = lanes_of(n * SMALL, SMALL)

            def part(rows):
                return ht[rows, cols].astype(F32), dat[rows, cols].astype(BF16).astype(F32)

            def sums(i, so_far):
                h, da = part(rows_of(i * LANES, LANES))
                return tuple(s + jnp.sum((v * h).reshape(-1, 8, SMALL), 0) for s, v in zip(so_far, (h, da)))

            none = jnp.zeros((8, SMALL), F32)
            square, cross = (jnp.sum(v, 0, keepdims=True) for v in lax.fori_loop(0, d // LANES, sums, (none, none)))
            scale = lax.rsqrt(square / d + 1e-6)
            h, da = part(ALL)
            v = dyt[:, cols].astype(F32) + scale * (da - h * scale * (scale * cross / d))
            v = v.astype(BF16)
            if not last:
                dyt[:, cols] = v
                dat[:, cols] = jnp.zeros((d, SMALL), F32)
            dy[cols, :] = v.T
            return carry

        with jax.named_scope("end"):
            lax.fori_loop(begin // SMALL, end // SMALL, chunk, 0)

    def keep(k):
        return copies([(v, kept_h.at[n, k - nb]) for n, v in enumerate((dg, du))], ksem)

    def load_f(q):
        rows = rows_of(q % QUARTERS * BLOCK, BLOCK)
        return copies([(f_h.at[e, q // QUARTERS, rows, :], f.at[slot3(q), e]) for e in PAIR], fsem.at[slot3(q)])

    def load_act(k):
        return pltpu.make_async_copy(act_h.at[k - nb], act, ksem.at[2])

    def compute(k, between):
        slot = odd(k)
        wait((load_up(k), *load_down(k)))

        def chunk(n, carry):
            for part in PARTS:
                rows = rows_of(n * BIG + part.start, BLOCK)
                for cols in COLUMNS:
                    g = dot(a[rows, :], wup[slot, 0, :, cols])
                    u = dot(a[rows, :], wup[slot, 1, :, cols])
                    e = dot_t(dy[rows, :], wd[slot, cols, :]).astype(BF16).astype(F32)
                    sig, s = gate(g)
                    act[rows, cols] = (s * u).astype(BF16)
                    dg[rows, cols] = (e * u * (sig + s - s * sig)).astype(BF16)
                    du[rows, cols] = (e * s).astype(BF16)

            @pl.when(n == 0)
            def _():
                between()

            return carry

        lax.fori_loop(0, tokens // BIG, chunk, 0)

    def compute_last(k):
        slot = odd(k)
        wait((load_up(k), *load_down(k)))

        @pl.when(k > nb)
        def _():
            wait(keep(k - 1))

        def chunk(n, carry):
            q = (k - nb) * QUARTERS + n
            wait(load_f(q))

            @pl.when(q + 2 < nb * QUARTERS)
            def _():
                start(load_f(q + 2))

            for cols in COLUMNS:
                e = dot_t(dy[rows_of(n * BLOCK, BLOCK), :], wd[slot, cols, :]).astype(BF16).astype(F32)
                for n_, v in enumerate((du, dg)):
                    v[rows_of(n * BLOCK, BLOCK), cols] = (e * f[slot3(q), n_, :, cols]).astype(BF16)
            return carry

        lax.fori_loop(0, tokens // BLOCK, chunk, 0)
        @pl.when(k < steps - 1)
        def _():
            start(keep(k))

    def terms(k, n, before=None):
        slot = slot3(k)
        if n < 2:
            for cols in (slice(0, SMALL), slice(SMALL, BLOCK)):
                tu[slot, n, :, cols] = dot(at[...], (dg, du)[n][:, cols]).astype(BF16)
            reduce.pair_up(k, n)
        else:
            @pl.when(k >= nb)
            def _():
                load_act(k).wait()

            for cols in (slice(0, SMALL), slice(SMALL, BLOCK)):
                td[slot, cols, :] = dot(dyt[...], act[:, cols]).astype(BF16).T
            before()
            reduce.pair_down(k)

    def back(k):
        slot = odd(k)
        for n in range(tokens // BLOCK):
            cols = pl.ds(n * BLOCK, BLOCK)
            dat[:, cols] += dot_t(wup[slot, 0], dg[cols, :]) + dot_t(wup[slot, 1], du[cols, :])

    def back_half(half, slot, first):
        rows, cols = rows_of(first, BIG), lanes_of(half * BIG, BIG)
        dat[:, cols] += dot_t(wup[slot, 0], dg[rows, :]) + dot_t(wup[slot, 1], du[rows, :])

    def later(t):
        half = jnp.where(t == 2, 0, 1)
        j = jnp.where(t == 2, nb - 2, t - 3)
        _, order, _ = gather.piece(j)
        slot = odd(t)
        yield pltpu.make_async_copy(wup_h.at[0, order], wup.at[slot], wsem.at[slot, 0])
        for n, v in enumerate((dg, du), 1):
            yield pltpu.make_async_copy(kept_h.at[n - 1, j, rows_of(half * BIG, BIG), :], v.at[rows_of(slot * BIG, BIG), :], wsem.at[slot, n])

    def back_later(t):
        @pl.when(t >= 2)
        def _():
            wait(later(t))

        @pl.when((t >= 1) & (t < nb + 1))
        def _():
            start(later(t + 1))

        slot = odd(t)
        back_half(jnp.where((t == 0) | (t == 2), 0, 1), jnp.where(t == 0, 1, slot), slot * BIG)

    def done(half):
        rows = pl.ds(half * BIG, BIG)
        return pltpu.make_async_copy(dy.at[rows, :], dx_h.at[rows, :], io.at[half])

    def step(k, carry):
        t = k - steps

        def stage(run, lag, *late):
            b = k - lag
            now = (k >= lag) & (k < steps)
            for n, when in enumerate(late):
                now = now | (t == when)
                b = jnp.where(t == when, steps - len(late) + n, b)

            @pl.when(now)
            def _():
                with jax.named_scope("r_" + run.__name__):
                    run(b)

        def tick(*entries):
            for group, when, run in entries:

                @pl.when(k == when)
                def _():
                    with jax.named_scope(f"gather_{group}_{when}"):
                        for i in (range(ahead, ahead + 2), range(ahead + 2, steps))[group]:
                            run(i)

        def arrived(i):
            wait_for(gather.units(36), dr.at[i])

        tick((0, 0, gather.first), (1, 3, gather.fourth))

        def between():
            stage(reduce.third, 2)

        @pl.when(k < nb)
        def _():
            with jax.named_scope("compute"):
                compute(k, between)

        @pl.when((k >= nb) & (k < steps))
        def _():
            with jax.named_scope("compute_last"):
                compute_last(k)

        tick((0, 0, gather.second), (0, 1, gather.fourth), (1, 1, gather.second), (1, 2, gather.third))

        @pl.when((k >= nb - 1) & (k + 1 < steps))
        def _():
            start((load_up(k + 1), *load_down(k + 1)))

        @pl.when(k >= nb)
        def _():
            stage(reduce.third, 2, 2, 5)

        stage(reduce.first, 1, 1)

        @pl.when(k == 0)
        def _():
            wait(loads[2:])

        def terms_of(n, before=None):
            @pl.when(k < steps)
            def _():
                with jax.named_scope(f"terms_{n}"):
                    terms(k, n, before)

        terms_of(0)
        terms_of(1)
        terms_of(2, lambda: stage(reduce.fourth, 2))

        @pl.when(k >= steps)
        def _():
            stage(reduce.fourth, steps, 4, nb)

        stage(reduce.second, 1, 3)
        tick((0, 0, gather.third), (1, 0, gather.first), (0, 1, arrived), (1, 3, arrived))

        @pl.when((k >= nb - 1) & (k + 1 < steps))
        def _():
            load_act(k + 1).start()

        @pl.when(k < nb - 1)
        def _():
            start((load_up(k + 1), *load_down(k + 1)))

        @pl.when(k < nb)
        def _():
            with jax.named_scope("back"):
                back(k)

        @pl.when((k >= nb) & (k < steps - 2))
        def _():
            with jax.named_scope("back_half"):
                back_half(0, odd(k), 0)

        @pl.when(k == nb - 1)
        def _():
            load = pltpu.make_async_copy(a0t_h, at, io.at[0])
            start((load, *load_f(0), *load_f(1)))
            layer_end(0, tokens, False)
            turned.start()
            load.wait()

        @pl.when((t >= 0) & (t < nb + 2))
        def _():
            with jax.named_scope("back_later"):
                back_later(t)

        @pl.when(t == 2)
        def _():
            turned.wait()
            layer_end(0, BIG, True)
            done(0).start()

        return carry

    turned = pltpu.make_async_copy(xt_h, ht, io.at[4])
    lax.fori_loop(0, steps + nb + 2, step, 0)
    layer_end(BIG, tokens, True)
    done(1).start()

    def drain(i, carry):
        gather.sent(i, 12)
        return carry

    lax.fori_loop(ahead, steps, drain, 0)
    for two in PAIR:
        reduce.final_sent(two)
    reduce.wait(6 * steps, ru.at[0])
    reduce.wait(48, rd.at[0])
    wait((done(0), done(1)))


def backward(mesh, dy, dyt, a0t, xt, a1, a1t, h1t, f, act, wup, wd):
    nr, ns = mesh.shape["r"], mesh.shape["s"]
    nx = ns // 2
    tokens, d = dy.shape
    layers, nb = wup.shape[:2]
    hidden = nb * BLOCK
    m, share, rows = d // ns, hidden // ns, BLOCK // ns
    outs = (array(tokens, d), array(2, layers, m, hidden), array(layers, share, d), array(*wup.shape), array(*wd.shape), array(2, nb, tokens, BLOCK))
    scratch = [
        *[vmem(tokens, d), vmem(d, tokens)] * 2, vmem(d, tokens), vmem(d, tokens, dtype=F32), vmem(3, 2, BLOCK, BLOCK, dtype=F32), *[vmem(tokens, BLOCK)] * 3,
        vmem(2, 2, d, BLOCK), vmem(2, BLOCK, d), vmem(3, 2, d, BLOCK), vmem(3, BLOCK, d), vmem(3, nx, 2, m, BLOCK), vmem(3, nx, rows, d),
        vmem(2, 2, 2, m, BLOCK // 2), vmem(2, 2, rows // 2, d), vmem(3, 2, 2, m, BLOCK), vmem(3, 2, rows, d),
        vmem(2, nr - 1, 2, m, LANES), vmem(2, nr - 1, rows // QUARTERS, d), vmem(2, 2, m, LANES), vmem(2, rows // QUARTERS, d),
        *sems(3, 3, 2, (2, 2), 3, (3, 2), 2, (2, nr - 1), 2, 2, 2, 1, 1), *gather_sems(layers * nb), *sems(5, (QUARTERS, QUARTERS), 3, (3, 2)),
    ]
    return call(backward_kernel, mesh, "backward", 1, outs, scratch, (dy, dyt, a0t, xt, a1, a1t, h1t, f, act, wup, wd), {9: 3, 10: 4})[:3]


def deliver_kernel(nr, ns, dx_h, gup_h, gd_h, out_x, out_gate, out_up, out_down, x, up, down, arrive, leave):
    jobs = []
    for h, out, v in ((dx_h, out_x, x), (gup_h.at[0], out_gate, up.at[0]), (gup_h.at[1], out_up, up.at[1]), (gd_h, out_down, down)):
        size = BIG if out is out_x else 1
        for n in range(0, out.shape[0], size):
            part = pl.ds(n, size)
            jobs.append((h.at[part], v.at[part], out.at[part]))
    loads = copies([job[:2] for job in jobs], arrive)
    stores = copies([job[1:] for job in jobs], leave)
    start(loads)
    for load, store in zip(loads, stores):
        load.wait()
        store.start()
    wait(stores)


def deliver(mesh, dx, gup, gd):
    up = gup.shape[1:]
    scratch = [vmem(*v.shape) for v in (dx, gup, gd)] + sems(8, 8)
    return call(deliver_kernel, mesh, "deliver", None, (array(*dx.shape), array(*up), array(*up), array(*gd.shape)), scratch, (dx, gup, gd))


def solution(mesh):
    def step(x, dy, *weights):
        xt, dyt, a0t, a1, a1t, h1t, wup, wd, f, act = forward(mesh, x[0], dy[0], *weights)
        results = backward(mesh, dy[0], dyt, a0t, xt, a1, a1t, h1t, f, act, wup, wd)
        dx, *by_weights = deliver(mesh, *results)
        return dx[None], *by_weights

    states, cut = P(("rep", "r", "s"), None, None), P(None, "s", None)
    return jax.shard_map(
        step,
        mesh=mesh,
        in_specs=(states, states) + (cut,) * 3,
        out_specs=(states,) + (P("rep", "s", None),) * 3,
        check_vma=False,
    )
```

time: 748 us -> 375 us (0.50)
  matrix products: 429 us -> 0 us
  Pallas kernels: 0 us -> 374 us
  waiting for transfers between devices: 252 us -> 0 us
  local copies, waits for them, and re-layouts: 27.4 us -> 0 us
  other arithmetic: 16.9 us -> 0 us
  between operations: 14.5 us -> 0.81 us
    dot_general x17 -> x0, matrix products: 429 us -> none  [the longest x6 152 us: layer(): up = jnp.dot(a, w['w_up'], preferred_element_type=jnp.float32)]
    pallas_call x0 -> x3, Pallas kernels: none -> 374 us  [call(): pl.pallas_call(functools.partial(kernel, mesh.shape['r'], mesh.shape['s']...]
    reduce_scatter x6 -> x0, waiting for transfers between devices: 104 us -> none  [summed(): lax.psum_scatter(term, 's', scatter_dimension=0, tiled=True)]
    all_gather x6 -> x0, waiting for transfers between devices: 98.6 us -> none  [fetched(): lax.all_gather(w[number], 's', axis=0, tiled=True)]
    psum x1 -> x0, waiting for transfers between devices: 47.1 us -> none  [summed(): lax.psum(lax.psum_scatter(term, 's', scatter_dimension=0, tiled=True), 'r')]
    unnamed x31 -> x0, local copies, waits for them, and re-layouts: 20.7 us -> none
  transfers between devices with their start and end apart: 13 -> 0, of which waited for: 10 -> 0; matrix products, arithmetic and copies ran while one was open for 48% -> 0% of each run, Pallas kernels for 0% -> 0%
where the time goes in v3:
time: 375 us
  Pallas kernels  374 us (100%)
    pallas_call x3, Pallas kernels, call(): pl.pallas_call(functools.partial(kernel, mesh.shape['r'], mesh.shape['s']...  374 us

profile of v3, /device:TPU:97, one launch (start us, length us, event | category | flops | bytes accessed | tf_op | source)
XLA Modules:
  0.0 374.8 jit_solution(5840797667079959970)
XLA Ops:
  0.6 96.5 %forward.1 = (bf16[896,2048]{1,0:T(8,128)(2,1)}, bf16[896,2048]{1,0:T(8,128)(2,1)}, bf16[896,2048]{1,0:T(8,128)(2,1)}, bf16[2048,896]{1,0:T(8,128)(2,1)}, bf16[8...) custom-call(bf16[2048,896]{1,0:T(8,128)(2,1)} %bitcast.5, ...), custom_call_target="tpu_custom_call" | custom-call | tf_op jit(solution)/shard_map/forward/pallas_call | solution.py:427
  97.1 270.6 %backward.1 = (bf16[2048,896]{1,0:T(8,128)(2,1)}, bf16[2,2,112,3584]{3,2,1,0:T(8,128)(2,1)}, bf16[2,448,896]{2,1,0:T(8,128)(2,1)}, bf16[2,7,2,896,512]{4,3,2,1,0...) custom-call(bf16[2048,896]{1,0:T(8,128)(2,1)} %bitcast.4, ...), custom_call_target="tpu_custom_call", output_to_operand_aliasing={{3}: (9, {}), {4}: (10, {})} | custom-call | tf_op jit(solution)/shard_map/backward/pallas_call | solution.py:427
  367.8 6.8 %deliver.1 = (bf16[2048,896]{1,0:T(8,128)(2,1)}, bf16[2,112,3584]{2,1,0:T(8,128)(2,1)}, bf16[2,112,3584]{2,1,0:T(8,128)(2,1)}, bf16[2,448,896]{2,1,0:T(8,128)(2,1)}) custom-call(bf16[2048,896]{1,0:T(8,128)(2,1)} %get-tuple-element.31.dx_h, bf16[2,2,112,3584]{3,2,1,0:T(8,128)(2,1)} %get-tuple-element.32.gup_h, bf16[2,448,896]{2,1,0:T(8,128)(2,1)} %get-tuple-element.33.gd_h), custom_call_target="tpu_custom_call" | custom-call | tf_op jit(solution)/shard_map/deliver/pallas_call | solution.py:427

commit v4 on v3

--- a/solution.py
+++ b/solution.py
@@ -212,13 +212,15 @@
     own = (oup, od)
     gather = Gather(place, (wup_h, wd_h), oup.shape[2], od.shape[1], (x1s, x1r, x2s, x2r, ys, yr, ds, dr, loc))
 
-    def prepare(k, carry):
-        rows = rows_of(k * SMALL, SMALL)
-        h = x[rows, :]
+    def norm_rows(rows, h):
         n = normed(h.astype(F32)).astype(BF16)
         a[rows, :] = n
         t3[:, rows] = n.T
         t1[:, rows] = h.T
+
+    def prepare(k, carry):
+        rows = rows_of(k * SMALL, SMALL)
+        norm_rows(rows, x[rows, :])
         return carry
 
     def turn(k, carry):
@@ -323,20 +325,14 @@
     with jax.named_scope("ready"):
         ready(0)
     load_up(0).start()
-    last = pieces - 2
-
     def step(i, carry):
         def between():
             with jax.named_scope("gather"):
                 for n, run in enumerate((gather.fourth, gather.third, gather.second, begin), 1):
 
-                    @pl.when(i + n <= last)
+                    @pl.when(i + n < pieces)
                     def _():
                         run(i + n)
-
-                    @pl.when(i + n == last)
-                    def _():
-                        run(last + 1)
 
                 @pl.when(pieces + i < every)
                 def _():
@@ -366,6 +362,7 @@
         return carry
 
     lax.fori_loop(0, nb, step, 0)
+    gather.fourth(pieces - 1)
     wait((*outs, *load_down(nb - 1)))
     start((*keep(nb - 1, 1), keep_act(nb - 1)))
     finals = ((a, a1_h, 0), (t3, a1t_h, 1), (t1, h1t_h, 1))
@@ -374,11 +371,7 @@
         for e in PAIR:
             rows = rows_of((2 * k + e) * SMALL, SMALL)
             y = acc[rows, :] + dot(act[(nb - 1) % 2, rows, :], wd[(nb - 1) % 2])
-            h = (x[rows, :].astype(F32) + y.astype(BF16).astype(F32)).astype(BF16)
-            n = normed(h.astype(F32)).astype(BF16)
-            a[rows, :] = n
-            t3[:, rows] = n.T
-            t1[:, rows] = h.T
+            norm_rows(rows, (x[rows, :].astype(F32) + y.astype(BF16).astype(F32)).astype(BF16))
         rows = rows_of(2 * k * SMALL, 2 * SMALL)
         for n, (p, q, dim) in enumerate(finals):
             part = (ALL,) * dim + (rows,)
@@ -470,10 +463,10 @@
     def wait(self, n, sem):
         wait_for(units(self.like, self.m, n), sem)
 
-    def pair_up(self, b, k):
+    def pair_up(self, b):
         slot, other = slot3(b), 1 - self.p.c
         for x in range(self.p.nx):
-            send(self.tu.at[slot, k, self.own_rows(x, other), :], self.pu.at[slot, x, k], self.ps.at[slot], self.pr.at[slot], self.p.at(dc=1))
+            send(self.tu.at[slot, :, self.own_rows(x, other), :], self.pu.at[slot, x], self.ps.at[slot], self.pr.at[slot], self.p.at(dc=1))
 
     def pair_down(self, b):
         slot, other = slot3(b), 1 - self.p.c
@@ -596,7 +589,8 @@
     tokens, d = a.shape
     layers, nb = wup_h.shape[:2]
     steps = layers * nb
-    loads = copies(((a1_h, a), (dy_h, dy), (a1t_h, at), (dyt_h, dyt), (h1t_h, ht)), io)
+    halves = [(h.at[pl.ds(n, BIG), :], v.at[pl.ds(n, BIG), :]) for n in range(0, tokens, BIG) for h, v in ((a1_h, a), (dy_h, dy))]
+    loads = copies(halves + [(a1t_h, at), (dyt_h, dyt), (h1t_h, ht)], io)
     gather = Gather(place, (wup_h, wd_h), gup_h.shape[2], gd_h.shape[1], (x1s, x1r, x2s, x2r, ys, yr, ds, dr, None))
     ahead = nb + AHEAD
 
@@ -611,7 +605,7 @@
         layer, j, _ = block_of(b)
         return copies([(wd_h.at[layer, rows_of((q * nb + j) * LANES, LANES), :], wd.at[odd(b), pl.ds(q * LANES, LANES), :]) for q in range(QUARTERS)], wsem.at[2 + odd(b)])
 
-    start((*loads[:2], load_up(0), *load_down(0)))
+    start((*loads[:2], load_up(0), *load_down(0), *loads[2:4]))
     greet([place.at(dc=1)] + [place.at(dx=hop) for hop in HOPS] + [place.at(dy=hop, dc=c) for hop in range(1, nr) for c in CORES])
     reduce = Reduce(
         place, wup_h.at[0, :, 0], nb, layers, (tu, td, pu, pd, h1u, h1d, h2u, h2d, su, sd, fu, fd), (gup_h, gd_h),
@@ -619,7 +613,6 @@
     )
     dat[...] = jnp.zeros_like(dat)
     wait(loads[:2])
-    start(loads[2:])
 
     def layer_end(begin, end, last):
         def chunk(n, carry):
@@ -708,21 +701,21 @@
         def _():
             start(keep(k))
 
-    def terms(k, n, before=None):
+    def terms(k, before):
         slot = slot3(k)
-        if n < 2:
-            for cols in (slice(0, SMALL), slice(SMALL, BLOCK)):
-                tu[slot, n, :, cols] = dot(at[...], (dg, du)[n][:, cols]).astype(BF16)
-            reduce.pair_up(k, n)
-        else:
-            @pl.when(k >= nb)
-            def _():
-                load_act(k).wait()
-
-            for cols in (slice(0, SMALL), slice(SMALL, BLOCK)):
-                td[slot, cols, :] = dot(dyt[...], act[:, cols]).astype(BF16).T
-            before()
-            reduce.pair_down(k)
+
+        @pl.when(k >= nb)
+        def _():
+            load_act(k).wait()
+
+        for cols in COLUMNS:
+            td[slot, cols, :] = dot(dyt[...], act[:, cols]).astype(BF16).T
+        for n, left in enumerate((dg, du)):
+            for cols in COLUMNS:
+                tu[slot, n, :, cols] = dot(at[...], left[:, cols]).astype(BF16)
+        reduce.pair_up(k)
+        before()
+        reduce.pair_down(k)
 
     def back(k):
         slot = odd(k)
@@ -775,20 +768,27 @@
                     run(b)
 
         def tick(*entries):
-            for group, when, run in entries:
+            for pieces, when, run in entries:
 
                 @pl.when(k == when)
                 def _():
-                    with jax.named_scope(f"gather_{group}_{when}"):
-                        for i in (range(ahead, ahead + 2), range(ahead + 2, steps))[group]:
-                            run(i)
+                    with jax.named_scope("gather"):
+                        for i in pieces:
+                            run(ahead + i)
+
+        one, two, rest = (0,), (1,), range(2, steps - ahead)
 
         def arrived(i):
             wait_for(gather.units(36), dr.at[i])
 
-        tick((0, 0, gather.first), (1, 3, gather.fourth))
+        tick((one, 0, gather.first), (two, 0, gather.first), (one, 1, gather.fourth), (two, 1, gather.third), (rest, 3, gather.fourth))
 
         def between():
+            @pl.when(k == 0)
+            def _():
+                wait(loads[2:4])
+                start(loads[4:])
+
             stage(reduce.third, 2)
 
         @pl.when(k < nb)
@@ -801,7 +801,7 @@
             with jax.named_scope("compute_last"):
                 compute_last(k)
 
-        tick((0, 0, gather.second), (0, 1, gather.fourth), (1, 1, gather.second), (1, 2, gather.third))
+        tick((one, 0, gather.second), (two, 1, gather.fourth), (rest, 2, gather.third))
 
         @pl.when((k >= nb - 1) & (k + 1 < steps))
         def _():
@@ -815,24 +815,19 @@
 
         @pl.when(k == 0)
         def _():
-            wait(loads[2:])
-
-        def terms_of(n, before=None):
-            @pl.when(k < steps)
-            def _():
-                with jax.named_scope(f"terms_{n}"):
-                    terms(k, n, before)
-
-        terms_of(0)
-        terms_of(1)
-        terms_of(2, lambda: stage(reduce.fourth, 2))
+            wait(loads[4:])
+
+        @pl.when(k < steps)
+        def _():
+            with jax.named_scope("terms"):
+                terms(k, lambda: stage(reduce.fourth, 2))
 
         @pl.when(k >= steps)
         def _():
             stage(reduce.fourth, steps, 4, nb)
 
         stage(reduce.second, 1, 3)
-        tick((0, 0, gather.third), (1, 0, gather.first), (0, 1, arrived), (1, 3, arrived))
+        tick((one, 0, gather.third), (two, 0, gather.second), (rest, 0, gather.first), ((0, 1), 1, arrived), (rest, 1, gather.second), (rest, 3, arrived))
 
         @pl.when((k >= nb - 1) & (k + 1 < steps))
         def _():
@@ -903,7 +898,7 @@
         vmem(2, 2, d, BLOCK), vmem(2, BLOCK, d), vmem(3, 2, d, BLOCK), vmem(3, BLOCK, d), vmem(3, nx, 2, m, BLOCK), vmem(3, nx, rows, d),
         vmem(2, 2, 2, m, BLOCK // 2), vmem(2, 2, rows // 2, d), vmem(3, 2, 2, m, BLOCK), vmem(3, 2, rows, d),
         vmem(2, nr - 1, 2, m, LANES), vmem(2, nr - 1, rows // QUARTERS, d), vmem(2, 2, m, LANES), vmem(2, rows // QUARTERS, d),
-        *sems(3, 3, 2, (2, 2), 3, (3, 2), 2, (2, nr - 1), 2, 2, 2, 1, 1), *gather_sems(layers * nb), *sems(5, (QUARTERS, QUARTERS), 3, (3, 2)),
+        *sems(3, 3, 2, (2, 2), 3, (3, 2), 2, (2, nr - 1), 2, 2, 2, 1, 1), *gather_sems(layers * nb), *sems(8, (QUARTERS, QUARTERS), 3, (3, 2)),
     ]
     return call(backward_kernel, mesh, "backward", 1, outs, scratch, (dy, dyt, a0t, xt, a1, a1t, h1t, f, act, wup, wd), {9: 3, 10: 4})[:3]
 

time: 375 us -> 362 us (0.965)
  Pallas kernels: 374 us -> 361 us
    pallas_call x3, Pallas kernels: 374 us -> 361 us  [call(): pl.pallas_call(functools.partial(kernel, mesh.shape['r'], mesh.shape['s']...]
where the time goes in v4:
time: 362 us
  Pallas kernels  361 us (100%)
    pallas_call x3, Pallas kernels, call(): pl.pallas_call(functools.partial(kernel, mesh.shape['r'], mesh.shape['s']...  361 us

profile of v4, /device:TPU:97, one launch (start us, length us, event | category | flops | bytes accessed | tf_op | source)
XLA Modules:
  0.0 361.5 jit_solution(1208917317660285540)
XLA Ops:
  0.6 93.8 %forward.1 = (bf16[896,2048]{1,0:T(8,128)(2,1)}, bf16[896,2048]{1,0:T(8,128)(2,1)}, bf16[896,2048]{1,0:T(8,128)(2,1)}, bf16[2048,896]{1,0:T(8,128)(2,1)}, bf16[8...) custom-call(bf16[2048,896]{1,0:T(8,128)(2,1)} %bitcast.5, ...), custom_call_target="tpu_custom_call" | custom-call | tf_op jit(solution)/shard_map/forward/pallas_call | solution.py:420
  94.4 260.1 %backward.1 = (bf16[2048,896]{1,0:T(8,128)(2,1)}, bf16[2,2,112,3584]{3,2,1,0:T(8,128)(2,1)}, bf16[2,448,896]{2,1,0:T(8,128)(2,1)}, bf16[2,7,2,896,512]{4,3,2,1,0...) custom-call(bf16[2048,896]{1,0:T(8,128)(2,1)} %bitcast.4, ...), custom_call_target="tpu_custom_call", output_to_operand_aliasing={{3}: (9, {}), {4}: (10, {})} | custom-call | tf_op jit(solution)/shard_map/backward/pallas_call | solution.py:420
  354.5 6.8 %deliver.1 = (bf16[2048,896]{1,0:T(8,128)(2,1)}, bf16[2,112,3584]{2,1,0:T(8,128)(2,1)}, bf16[2,112,3584]{2,1,0:T(8,128)(2,1)}, bf16[2,448,896]{2,1,0:T(8,128)(2,1)}) custom-call(bf16[2048,896]{1,0:T(8,128)(2,1)} %get-tuple-element.31.dx_h, bf16[2,2,112,3584]{3,2,1,0:T(8,128)(2,1)} %get-tuple-element.32.gup_h, bf16[2,448,896]{2,1,0:T(8,128)(2,1)} %get-tuple-element.33.gd_h), custom_call_target="tpu_custom_call" | custom-call | tf_op jit(solution)/shard_map/deliver/pallas_call | solution.py:420

commit v5 on v4

--- a/solution.py
+++ b/solution.py
@@ -311,12 +311,9 @@
     def down(i):
         wait(load_down(i))
 
-        def chunk(n, carry):
-            rows = rows_of(n * BIG, BIG)
+        for n in range(tokens // BIG):
+            rows = pl.ds(n * BIG, BIG)
             acc[rows, :] += dot(act[odd(i), rows, :], wd[odd(i)])
-            return carry
-
-        lax.fori_loop(0, tokens // BIG, chunk, 0)
 
     def ready(i):
         wait_for(gather.units(48), dr.at[i])
@@ -807,11 +804,12 @@
         def _():
             start((load_up(k + 1), *load_down(k + 1)))
 
+        stage(reduce.first, 1, 1)
+
         @pl.when(k >= nb)
         def _():
-            stage(reduce.third, 2, 2, 5)
-
-        stage(reduce.first, 1, 1)
+            stage(reduce.third, 2, 2, 6)
+
 
         @pl.when(k == 0)
         def _():
@@ -824,7 +822,7 @@
 
         @pl.when(k >= steps)
         def _():
-            stage(reduce.fourth, steps, 4, nb)
+            stage(reduce.fourth, steps, 5, nb + 2)
 
         stage(reduce.second, 1, 3)
         tick((one, 0, gather.third), (two, 0, gather.second), (rest, 0, gather.first), ((0, 1), 1, arrived), (rest, 1, gather.second), (rest, 3, arrived))
@@ -860,18 +858,14 @@
             with jax.named_scope("back_later"):
                 back_later(t)
 
-        @pl.when(t == 2)
-        def _():
-            turned.wait()
-            layer_end(0, BIG, True)
-            done(0).start()
-
         return carry
 
     turned = pltpu.make_async_copy(xt_h, ht, io.at[4])
-    lax.fori_loop(0, steps + nb + 2, step, 0)
-    layer_end(BIG, tokens, True)
-    done(1).start()
+    lax.fori_loop(0, steps + nb + 3, step, 0)
+    turned.wait()
+    for half in PAIR:
+        layer_end(half * BIG, half * BIG + BIG, True)
+        done(half).start()
 
     def drain(i, carry):
         gather.sent(i, 12)

time: 362 us -> 360 us (level)
  no operation moved by 1% of the time
where the time goes in v5:
time: 360 us; the launch traced here: 359 us
  Pallas kernels  358 us (99%)
    pallas_call x3, Pallas kernels, call(): pl.pallas_call(functools.partial(kernel, mesh.shape['r'], mesh.shape['s']...  358 us

profile of v5, /device:TPU:97, one launch (start us, length us, event | category | flops | bytes accessed | tf_op | source)
XLA Modules:
  0.0 359.2 jit_solution(2244768522738326270)
XLA Ops:
  0.6 93.3 %forward.1 = (bf16[896,2048]{1,0:T(8,128)(2,1)}, bf16[896,2048]{1,0:T(8,128)(2,1)}, bf16[896,2048]{1,0:T(8,128)(2,1)}, bf16[2048,896]{1,0:T(8,128)(2,1)}, bf16[8...) custom-call(bf16[2048,896]{1,0:T(8,128)(2,1)} %bitcast.5, ...), custom_call_target="tpu_custom_call" | custom-call | tf_op jit(solution)/shard_map/forward/pallas_call | solution.py:417
  93.9 258.3 %backward.1 = (bf16[2048,896]{1,0:T(8,128)(2,1)}, bf16[2,2,112,3584]{3,2,1,0:T(8,128)(2,1)}, bf16[2,448,896]{2,1,0:T(8,128)(2,1)}, bf16[2,7,2,896,512]{4,3,2,1,0...) custom-call(bf16[2048,896]{1,0:T(8,128)(2,1)} %bitcast.4, ...), custom_call_target="tpu_custom_call", output_to_operand_aliasing={{3}: (9, {}), {4}: (10, {})} | custom-call | tf_op jit(solution)/shard_map/backward/pallas_call | solution.py:417
  352.2 6.8 %deliver.1 = (bf16[2048,896]{1,0:T(8,128)(2,1)}, bf16[2,112,3584]{2,1,0:T(8,128)(2,1)}, bf16[2,112,3584]{2,1,0:T(8,128)(2,1)}, bf16[2,448,896]{2,1,0:T(8,128)(2,1)}) custom-call(bf16[2048,896]{1,0:T(8,128)(2,1)} %get-tuple-element.31.dx_h, bf16[2,2,112,3584]{3,2,1,0:T(8,128)(2,1)} %get-tuple-element.32.gup_h, bf16[2,448,896]{2,1,0:T(8,128)(2,1)} %get-tuple-element.33.gd_h), custom_call_target="tpu_custom_call" | custom-call | tf_op jit(solution)/shard_map/deliver/pallas_call | solution.py:417
